TPU v7x, 32 devices: a whole 2x2x4 slice. The times are simulated.
32 devices in a mesh: band: 4 (over y, core), grid: 8 (over z, x).
Axes of the slice: x: 2, y: 2, z: 4, core: 2. Of those that a mesh axis runs over, the one named last changes fastest.
Arguments:
- orbitals: bfloat16 [64, 2, 16, 128, 128], P('band', None, 'grid'), may hold values from -1.5 to 1.5
- occupations: float32 [64], P('band'), may hold values from 0.2 to 2
Outputs:
- current: float32 [3, 16, 128, 128], P(None, 'grid', 'band')
All inputs are finite; a program needn't handle non-finite values.
Results may differ from a plain program's by a relative error of at most 0.0003.
Values may be sent and summed in bfloat16 or wider, within the bound.
A program may use at most 64 MiB of HBM per device.

v0:
```python
import functools

import jax
import jax.numpy as jnp
from jax import lax
from jax.experimental import pallas as pl
from jax.experimental.pallas import tpu as pltpu
from jax.sharding import PartitionSpec as P

CHUNK = 16


def stencil(n, flipped):
    row = lax.broadcasted_iota(jnp.int32, (n, n), 0)
    col = lax.broadcasted_iota(jnp.int32, (n, n), 1)
    d = col - row if flipped else row - col
    value = jnp.zeros((n, n), jnp.float32)
    for step, weight in ((1, 8.0), (-1, -8.0), (2, -1.0), (-2, 1.0)):
        hit = (d == step) | (d == step - n) | (d == step + n)
        value = jnp.where(hit, weight, value)
    return value.astype(jnp.bfloat16)


def kernel(
    nb, ng, occ_ref, orb_ref, out_ref,
    own, mate, outer, mx, my, plane_sum, plane_recv, zsend, zrecv,
    own_sem, mate_send, mate_recv, outer_send, outer_recv,
    plane_send_sem, plane_recv_sem, z_send_sem, z_recv_sem, ready,
):
    bands, _, depth, nx, ny = orb_ref.shape
    b = lax.axis_index("band")
    g = lax.axis_index("grid")
    odd = lax.rem(g, 2)
    turn = 1 - 2 * odd
    partner = g + turn
    ahead = lax.rem(g + 2 * turn + ng, ng)
    behind = lax.rem(g - 2 * turn + ng, ng)
    rows = nx // nb
    subs = rows // CHUNK
    chunks = (nb // 2) * subs

    load = pltpu.make_async_copy(orb_ref, own, own_sem)
    load.start()

    barrier = pltpu.get_barrier_semaphore()
    peers = [lax.rem(b + k, nb) for k in range(1, nb)]
    direct = [(b, partner), (b, ahead), (b, behind)] + [(peer, g) for peer in peers]
    for band, grid in direct:
        pl.semaphore_signal(barrier, inc=1, device_id={"band": band, "grid": grid})
    pl.semaphore_wait(barrier, len(direct))

    def start_of(chunk, parity):
        block = (chunk // subs) * 2 + parity
        return pl.multiple_of(block * rows + (chunk % subs) * CHUNK, CHUNK)

    def to_mate(c):
        return pltpu.make_async_remote_copy(
            src_ref=orb_ref.at[:, :, :, pl.ds(start_of(c, 1 - odd), CHUNK), :],
            dst_ref=mate.at[c],
            send_sem=mate_send.at[c],
            recv_sem=mate_recv.at[c],
            device_id={"band": b, "grid": partner},
        )

    def to_outer(c):
        return pltpu.make_async_remote_copy(
            src_ref=orb_ref.at[:, :, :, pl.ds(start_of(c, odd), CHUNK), :],
            dst_ref=outer.at[c],
            send_sem=outer_send.at[c],
            recv_sem=outer_recv.at[c],
            device_id={"band": b, "grid": behind},
        )

    for c in range(chunks):
        to_mate(c).start()
        to_outer(c).start()
    for peer in peers:
        pl.semaphore_signal(ready, inc=1, device_id={"band": peer, "grid": g})

    mx[...] = stencil(nx, True)
    my[...] = stencil(ny, False)
    plane_sum[...] = jnp.zeros_like(plane_sum)
    load.wait()

    def lateral(n, carry):
        w = occ_ref[n]
        for s in range(depth):
            re = own[n, 0, s]
            im = own[n, 1, s]
            tx = jnp.dot(mx[...], jnp.concatenate([re, im], 1), preferred_element_type=jnp.float32)
            ty = jnp.dot(jnp.concatenate([re, im], 0), my[...], preferred_element_type=jnp.float32)
            wre = re.astype(jnp.float32) * w
            wim = im.astype(jnp.float32) * w
            plane_sum[0, s] += wre * tx[:, ny:] - wim * tx[:, :ny]
            plane_sum[1, s] += wre * ty[nx:] - wim * ty[:nx]
        return carry

    lax.fori_loop(0, bands, lateral, 0)

    def to_peer(k):
        peer = lax.rem(b + k, nb)
        return pltpu.make_async_remote_copy(
            src_ref=plane_sum.at[:, :, pl.ds(pl.multiple_of(peer * rows, rows), rows), :],
            dst_ref=plane_recv.at[k - 1],
            send_sem=plane_send_sem.at[k - 1],
            recv_sem=plane_recv_sem.at[k - 1],
            device_id={"band": peer, "grid": g},
        )

    for k in range(1, nb):
        to_peer(k).start()

    pl.semaphore_wait(ready, nb - 1)
    sign = turn.astype(jnp.float32)
    first = odd
    second = 1 - odd

    def to_owner(c, slab):
        at = (g, partner, ahead)[slab]
        sub = c % subs
        return pltpu.make_async_remote_copy(
            src_ref=zsend.at[c, slab],
            dst_ref=zrecv.at[slab // 2, b, :, pl.ds(sub * CHUNK, CHUNK), :],
            send_sem=z_send_sem.at[c, slab],
            recv_sem=z_recv_sem.at[slab // 2, b, sub],
            device_id={"band": (c // subs) * 2 + odd, "grid": at},
        )

    for c in range(chunks):
        if c == chunks - 1:
            mine = pl.ds(pl.multiple_of(b * rows, rows), rows)
            summed = plane_sum[:, :, mine, :]
            for k in range(1, nb):
                to_peer(k).wait_recv()
                summed = summed + plane_recv[k - 1]
            out_ref[1:3] = summed * (1.0 / 12.0)
        start = start_of(c, odd)
        to_mate(c).wait_recv()
        to_outer(c).wait_recv()

        def depthwise(n, sums):
            w = occ_ref[n] * sign
            fields = []
            for p in (first, second):
                fields.append(tuple(own[n, q, p, pl.ds(start, CHUNK), :].astype(jnp.float32) for q in (0, 1)))
            for held in (mate, outer):
                for p in (first, second):
                    fields.append(tuple(held[c, n, q, p].astype(jnp.float32) for q in (0, 1)))
            scaled = [(re * w, im * w) for re, im in fields[:4]]
            pairs = ((0, 1), (1, 2), (2, 3), (3, 4), (0, 2), (1, 3), (2, 4), (3, 5))
            return tuple(
                total + (scaled[i][0] * fields[j][1] - scaled[i][1] * fields[j][0])
                for total, (i, j) in zip(sums, pairs)
            )

        zero = jnp.zeros((CHUNK, ny), jnp.float32)
        n01, n12, n23, n34, f02, f13, f24, f35 = lax.fori_loop(0, bands, depthwise, (zero,) * 8, unroll=4)
        parts = (
            (8.0 * n01 - f02, 8.0 * (n01 + n12) - f13),
            (8.0 * (n12 + n23) - f02 - f24, 8.0 * (n23 + n34) - f13 - f35),
            (8.0 * n34 - f24, -f35),
        )
        owner = (c // subs) * 2 + odd
        for slab in (1, 2, 0):
            zsend[c, slab, first] = parts[slab][0]
            zsend[c, slab, second] = parts[slab][1]
            if slab:
                to_owner(c, slab).start()
            else:
                @pl.when(owner != b)
                def _():
                    to_owner(c, 0).start()

                @pl.when(owner == b)
                def _():
                    here = pl.ds((c % subs) * CHUNK, CHUNK)
                    zrecv[0, b, first, here, :] = parts[0][0]
                    zrecv[0, b, second, here, :] = parts[0][1]

    def arrival(kind, source):
        for sub in range(subs):
            pltpu.make_async_remote_copy(
                src_ref=zsend.at[0, 0],
                dst_ref=zrecv.at[kind, source, :, pl.ds(sub * CHUNK, CHUNK), :],
                send_sem=z_send_sem.at[0, 0],
                recv_sem=z_recv_sem.at[kind, source, sub],
                device_id={"band": b, "grid": partner},
            ).wait_recv()

    alike = lax.rem(b, 2) == odd

    @pl.when(alike)
    def _():
        for source in range(nb):
            @pl.when(b != source)
            def _():
                arrival(0, source)
        for source in range(nb):
            arrival(1, source)
        out_ref[0] = (jnp.sum(zrecv[0], 0) + jnp.sum(zrecv[1], 0)) * (1.0 / 12.0)

    @pl.when(jnp.logical_not(alike))
    def _():
        for source in range(nb):
            arrival(0, source)
        out_ref[0] = jnp.sum(zrecv[0], 0) * (1.0 / 12.0)

    for k in range(1, nb):
        to_peer(k).wait_send()
    for c in range(chunks):
        to_mate(c).wait_send()
        to_outer(c).wait_send()
        to_owner(c, 1).wait_send()
        to_owner(c, 2).wait_send()

        @pl.when((c // subs) * 2 + odd != b)
        def _():
            to_owner(c, 0).wait_send()


def solution(mesh):
    nb = mesh.shape["band"]
    ng = mesh.shape["grid"]

    def per_device(orbitals, occupations):
        bands, _, depth, nx, ny = orbitals.shape
        rows = nx // nb
        if depth != 2 or nb % 2 or ng % 2 or ng < 4 or rows % CHUNK:
            raise ValueError("unsupported sizes")
        subs = rows // CHUNK
        chunks = (nb // 2) * subs
        f32, bf16 = jnp.float32, jnp.bfloat16
        dma = pltpu.SemaphoreType.DMA
        return pl.pallas_call(
            functools.partial(kernel, nb, ng),
            out_shape=jax.ShapeDtypeStruct((3, depth, rows, ny), f32),
            in_specs=[
                pl.BlockSpec(memory_space=pltpu.SMEM),
                pl.BlockSpec(memory_space=pl.ANY),
            ],
            out_specs=pl.BlockSpec(memory_space=pltpu.VMEM),
            scratch_shapes=[
                pltpu.VMEM((bands, 2, depth, nx, ny), bf16),
                pltpu.VMEM((chunks, bands, 2, depth, CHUNK, ny), bf16),
                pltpu.VMEM((chunks, bands, 2, depth, CHUNK, ny), bf16),
                pltpu.VMEM((nx, nx), bf16),
                pltpu.VMEM((ny, ny), bf16),
                pltpu.VMEM((2, depth, nx, ny), f32),
                pltpu.VMEM((nb - 1, 2, depth, rows, ny), f32),
                pltpu.VMEM((chunks, 3, depth, CHUNK, ny), f32),
                pltpu.VMEM((2, nb, depth, rows, ny), f32),
                dma,
                dma((chunks,)),
                dma((chunks,)),
                dma((chunks,)),
                dma((chunks,)),
                dma((nb - 1,)),
                dma((nb - 1,)),
                dma((chunks, 3)),
                dma((2, nb, subs)),
                pltpu.SemaphoreType.REGULAR,
            ],
            compiler_params=pltpu.CompilerParams(collective_id=0, has_side_effects=True, vmem_limit_bytes=55000 * 1024),
            name="current",
        )(occupations, orbitals)

    return jax.shard_map(
        per_device,
        mesh=mesh,
        in_specs=(P("band", None, "grid", None, None), P("band")),
        out_specs=P(None, "grid", "band", None),
        check_vma=False,
    )
```

profile of v0, /device:TPU:4, one launch (start us, length us, event | category | flops | bytes accessed | tf_op | source)
XLA Modules:
  0.0 35.5 jit_solution(3702988830566096770)
XLA Ops:
  0.0 0.0 copy-start
  0.0 0.7 %copy-done = f32[16]{0:T(128)S(1)} copy-done((f32[16]{0:T(128)S(1)}, f32[16]{0:T(128)}, u32[]{:S(2)}) %copy-start) | copy-done | bytes 88
  0.7 34.2 %current.1 = f32[3,2,32,128]{3,2,1,0:T(8,128)S(1)} custom-call(f32[16]{0:T(128)S(1)} %copy-done, bf16[16,2,2,128,128]{4,3,2,1,0:T(8,128)(2,1)} %orb_ref.1), custom_call_target="tpu_custom_call" | custom-call | tf_op jit(solution)/shard_map/current/pallas_call | solution.py:234
  34.8 0.6 %copy.4 = f32[3,2,32,128]{3,2,1,0:T(8,128)} copy(f32[3,2,32,128]{3,2,1,0:T(8,128)S(1)} %current.1) | data formatting | bytes 196608
Async XLA Ops:
  0.0 0.7 %copy-start = (f32[16]{0:T(128)S(1)}, f32[16]{0:T(128)}, u32[]{:S(2)}) copy-start(f32[16]{0:T(128)} %occ_ref.1) | copy-start | bytes 196
where the time goes:
time: 35.6 us; the launch traced here: 35.5 us
  Pallas kernels  34.2 us (96%)
  local copies, waits for them, and re-layouts  1.3 us (4%)
    pallas_call x1, Pallas kernels, per_device(): pl.pallas_call(functools.partial(kernel, nb, ng), out_shape=jax.ShapeDtyp...  34.2 us
    unnamed x3, local copies, waits for them, and re-layouts  1.3 us

commit v1 on v0

v1 whole, which is shorter than its diff:
```python
import functools

import jax
import jax.numpy as jnp
from jax import lax
from jax.experimental import pallas as pl
from jax.experimental.pallas import tpu as pltpu
from jax.sharding import PartitionSpec as P

TILE = 16
PAIRS = ((0, 1), (1, 2), (2, 3), (3, 4), (0, 2), (1, 3), (2, 4), (3, 5))


def stencil(n, flipped):
    row = lax.broadcasted_iota(jnp.int32, (n, n), 0)
    col = lax.broadcasted_iota(jnp.int32, (n, n), 1)
    d = col - row if flipped else row - col
    value = jnp.zeros((n, n), jnp.float32)
    for step, weight in ((1, 8.0), (-1, -8.0), (2, -1.0), (-2, 1.0)):
        hit = (d == step) | (d == step - n) | (d == step + n)
        value = jnp.where(hit, weight, value)
    return value.astype(jnp.bfloat16)


def kernel(
    nb, ng, occ_hbm, orb_ref, out_ref,
    occ_ref, own, mate, outer, inner, mx, my, plane_sum, plane_recv, zsend, inbox, final,
    occ_sem, own_sem, mate_send, mate_recv, outer_send, outer_recv, inner_send, inner_recv,
    plane_send_sem, plane_recv_sem, inbox_send, inbox_recv, final_send, final_recv, up_token, down_token,
):
    bands, _, depth, nx, ny = orb_ref.shape
    b = lax.axis_index("band")
    g = lax.axis_index("grid")
    odd = lax.rem(g, 2)
    turn = 1 - 2 * odd
    partner = g + turn
    ahead = lax.rem(g + 2 * turn + ng, ng)
    behind = lax.rem(g - 2 * turn + ng, ng)
    side = lax.rem(g - turn + ng, ng)
    layers = ng // 2
    layer = g // 2
    rows = nx // nb
    half = rows // 2
    chips = nb // 2
    chip = b // 2
    core = lax.rem(b, 2)

    load = pltpu.make_async_copy(orb_ref, own, own_sem)
    load.start()
    weights = pltpu.make_async_copy(occ_hbm, occ_ref, occ_sem)
    weights.start()

    barrier = pltpu.get_barrier_semaphore()
    peers = [lax.rem(b + k, nb) for k in range(1, nb)]
    pl.semaphore_signal(barrier, inc=1, device_id={"band": b, "grid": partner})
    for peer in peers:
        pl.semaphore_signal(barrier, inc=1, device_id={"band": peer, "grid": g})

    @pl.when(layer > 0)
    def _():
        pl.semaphore_signal(barrier, inc=1, device_id={"band": b, "grid": g - 2})

    @pl.when(layer < layers - 1)
    def _():
        pl.semaphore_signal(barrier, inc=1, device_id={"band": b, "grid": g + 2})

    ends = (layer == 0).astype(jnp.int32) + (layer == layers - 1).astype(jnp.int32)
    pl.semaphore_wait(barrier, nb + 2 - ends)

    def chunk_of(k):
        return 2 * lax.rem(chip + 1 + k % chips, chips) + k // chips

    def start_of(k, parity):
        return pl.multiple_of(chunk_of(k) * rows + parity * half, half)

    def to_mate(k):
        return pltpu.make_async_remote_copy(
            src_ref=orb_ref.at[:, :, :, pl.ds(start_of(k, 1 - odd), half), :],
            dst_ref=mate.at[k],
            send_sem=mate_send.at[k],
            recv_sem=mate_recv.at[k],
            device_id={"band": b, "grid": partner},
        )

    def to_outer(k):
        return pltpu.make_async_remote_copy(
            src_ref=orb_ref.at[:, :, :, pl.ds(start_of(k, odd), half), :],
            dst_ref=outer.at[k - chips],
            send_sem=outer_send.at[k - chips],
            recv_sem=outer_recv.at[k - chips],
            device_id={"band": b, "grid": behind},
        )

    def to_inner(k):
        return pltpu.make_async_remote_copy(
            src_ref=mate.at[k],
            dst_ref=inner.at[k],
            send_sem=inner_send.at[k],
            recv_sem=inner_recv.at[k],
            device_id={"band": b, "grid": ahead},
        )

    wraps = ((odd == 0) & (layer == 0)) | ((odd == 1) & (layer == layers - 1))
    for k in range(nb):
        to_mate(k).start()

    @pl.when(jnp.logical_not(wraps))
    def _():
        for k in range(chips, nb):
            to_outer(k).start()

    @pl.when(layer == 1)
    def _():
        pl.semaphore_signal(up_token, inc=1, device_id={"band": b, "grid": g + 2})

    @pl.when(layer == layers - 2)
    def _():
        pl.semaphore_signal(down_token, inc=1, device_id={"band": b, "grid": g - 2})

    @pl.when(layer >= 2)
    def _():
        pl.semaphore_wait(up_token, 1)

        @pl.when(layer < layers - 1)
        def _():
            pl.semaphore_signal(up_token, inc=1, device_id={"band": b, "grid": g + 2})

    @pl.when(layer <= layers - 3)
    def _():
        pl.semaphore_wait(down_token, 1)

        @pl.when(layer > 0)
        def _():
            pl.semaphore_signal(down_token, inc=1, device_id={"band": b, "grid": g - 2})

    @pl.when(wraps)
    def _():
        for k in range(chips, nb):
            to_outer(k).start()

    mx[...] = stencil(nx, True)
    my[...] = stencil(ny, False)
    plane_sum[...] = jnp.zeros_like(plane_sum)
    load.wait()
    weights.wait()

    def lateral(n, carry):
        w = occ_ref[n]
        for s in range(depth):
            re = own[n, 0, s]
            im = own[n, 1, s]
            tx = jnp.dot(mx[...], jnp.concatenate([re, im], 1), preferred_element_type=jnp.float32)
            ty = jnp.dot(jnp.concatenate([re, im], 0), my[...], preferred_element_type=jnp.float32)
            wre = re.astype(jnp.float32) * w
            wim = im.astype(jnp.float32) * w
            plane_sum[0, s] += wre * tx[:, ny:] - wim * tx[:, :ny]
            plane_sum[1, s] += wre * ty[nx:] - wim * ty[:nx]
        return carry

    lax.fori_loop(0, bands, lateral, 0)

    def to_peer(k):
        peer = lax.rem(b + k, nb)
        return pltpu.make_async_remote_copy(
            src_ref=plane_sum.at[:, :, pl.ds(pl.multiple_of(peer * rows, rows), rows), :],
            dst_ref=plane_recv.at[k - 1],
            send_sem=plane_send_sem.at[k - 1],
            recv_sem=plane_recv_sem.at[k - 1],
            device_id={"band": peer, "grid": g},
        )

    for k in range(1, nb):
        to_peer(k).start()

    for k in range(chips):
        to_mate(k).wait_recv()
        to_inner(k).start()

    mine = pl.ds(pl.multiple_of(b * rows, rows), rows)
    summed = plane_sum[:, :, mine, :]
    for k in range(1, nb):
        to_peer(k).wait_recv()
        summed = summed + plane_recv[k - 1]
    out_ref[1:3] = summed * (1.0 / 12.0)

    def depthwise(k):
        direct = k >= chips
        first = odd if direct else 1 - odd
        second = 1 - first
        sign = (turn if direct else -turn).astype(jnp.float32)
        start = start_of(k, odd)

        def at_home(n, q, p):
            return own[n, q, p, pl.ds(start, half), :].astype(jnp.float32)

        def at_mate(n, q, p):
            return mate[k, n, q, p].astype(jnp.float32)

        def at_far(n, q, p):
            return (outer[k - chips, n, q, p] if direct else inner[k, n, q, p]).astype(jnp.float32)

        chain = (at_home, at_mate, at_far) if direct else (at_mate, at_home, at_far)

        def step(n, sums):
            w = occ_ref[n] * sign
            fields = [tuple(held(n, q, p) for q in (0, 1)) for held in chain for p in (first, second)]
            scaled = [(re * w, im * w) for re, im in fields[:4]]
            return tuple(
                total + (scaled[i][0] * fields[j][1] - scaled[i][1] * fields[j][0])
                for total, (i, j) in zip(sums, PAIRS)
            )

        zero = jnp.zeros((half, ny), jnp.float32)
        n01, n12, n23, n34, f02, f13, f24, f35 = lax.fori_loop(0, bands, step, (zero,) * 8, unroll=4)
        parts = (
            (8.0 * n01 - f02, 8.0 * (n01 + n12) - f13),
            (8.0 * (n12 + n23) - f02 - f24, 8.0 * (n23 + n34) - f13 - f35),
            (8.0 * n34 - f24, -f35),
        )
        for role, part in enumerate(parts if direct else (parts[1], parts[0], parts[2])):
            zsend[k, role, first] = part[0]
            zsend[k, role, second] = part[1]

    def to_inbox(k):
        chunk = chunk_of(k)
        slot = lax.rem(b - 2 * (chunk // 2) - 2 + nb, nb)
        return pltpu.make_async_remote_copy(
            src_ref=zsend.at[k],
            dst_ref=inbox.at[slot],
            send_sem=inbox_send.at[k],
            recv_sem=inbox_recv.at[slot],
            device_id={"band": chunk, "grid": g},
        )

    def from_inbox(slot):
        return pltpu.make_async_remote_copy(
            src_ref=zsend.at[0],
            dst_ref=inbox.at[slot],
            send_sem=inbox_send.at[0],
            recv_sem=inbox_recv.at[slot],
            device_id={"band": b, "grid": partner},
        )

    def to_final(k, role):
        slot = (0, 1 + core, 3 + core)[role]
        at = (g, partner, ahead if k >= chips else side)[role]
        return pltpu.make_async_remote_copy(
            src_ref=zsend.at[k, role],
            dst_ref=final.at[slot],
            send_sem=final_send.at[k // chips, role],
            recv_sem=final_recv.at[slot],
            device_id={"band": 2 * chip + k // chips, "grid": at},
        )

    def from_final(slot):
        return pltpu.make_async_remote_copy(
            src_ref=zsend.at[0, 0],
            dst_ref=final.at[slot],
            send_sem=final_send.at[0, 0],
            recv_sem=final_recv.at[slot],
            device_id={"band": b, "grid": partner},
        )

    def arrive(k):
        to_mate(k).wait_recv()
        to_outer(k).wait_recv()

    def finish(k):
        kind = k // chips

        @pl.when(core == kind)
        def _():
            for slot in range(nb - 2):
                from_inbox(slot).wait_recv()
            zsend[k] = zsend[k] + sum(inbox[slot] for slot in range(nb - 2))

        @pl.when(core != kind)
        def _():
            to_final(k, 0).start()

        for role in (2, 1):
            to_final(k, role).start()

    for j in range(chips - 1):
        arrive(chips + j)
        depthwise(chips + j)
        to_inbox(chips + j).start()
        to_inner(j).wait_recv()
        depthwise(j)
        to_inbox(j).start()
    arrive(nb - 1)
    depthwise(nb - 1)
    finish(nb - 1)
    to_inner(chips - 1).wait_recv()
    depthwise(chips - 1)
    finish(chips - 1)

    near = pl.ds(pl.multiple_of(odd * half, half), half)
    away = pl.ds(pl.multiple_of((1 - odd) * half, half), half)
    for slot in range(5):
        from_final(slot).wait_recv()
    far = final[3] + final[4]
    home = final[0]
    across = final[1] + final[2]

    @pl.when(core == 1)
    def _():
        out_ref[0, :, near, :] = (zsend[nb - 1, 0] + home + far) * (1.0 / 12.0)
        out_ref[0, :, away, :] = across * (1.0 / 12.0)

    @pl.when(core == 0)
    def _():
        out_ref[0, :, near, :] = (zsend[chips - 1, 0] + home) * (1.0 / 12.0)
        out_ref[0, :, away, :] = (across + far) * (1.0 / 12.0)

    for k in range(1, nb):
        to_peer(k).wait_send()
    for k in range(nb):
        to_mate(k).wait_send()
    for k in range(chips):
        to_outer(chips + k).wait_send()
        to_inner(k).wait_send()
    for k in range(chips - 1):
        to_inbox(k).wait_send()
        to_inbox(chips + k).wait_send()
    for k in (chips - 1, nb - 1):
        to_final(k, 1).wait_send()
        to_final(k, 2).wait_send()

        @pl.when(core != k // chips)
        def _():
            to_final(k, 0).wait_send()


def solution(mesh):
    nb = mesh.shape["band"]
    ng = mesh.shape["grid"]

    def per_device(orbitals, occupations):
        bands, _, depth, nx, ny = orbitals.shape
        rows = nx // nb
        half = rows // 2
        if depth != 2 or nb % 2 or nb < 4 or ng % 2 or ng < 6 or half % TILE:
            raise ValueError("unsupported sizes")
        chips = nb // 2
        f32, bf16 = jnp.float32, jnp.bfloat16
        dma = pltpu.SemaphoreType.DMA
        return pl.pallas_call(
            functools.partial(kernel, nb, ng),
            out_shape=jax.ShapeDtypeStruct((3, depth, rows, ny), f32),
            in_specs=[
                pl.BlockSpec(memory_space=pltpu.HBM),
                pl.BlockSpec(memory_space=pltpu.HBM),
            ],
            out_specs=pl.BlockSpec(memory_space=pltpu.VMEM),
            scratch_shapes=[
                pltpu.SMEM((bands,), f32),
                pltpu.VMEM((bands, 2, depth, nx, ny), bf16),
                pltpu.VMEM((nb, bands, 2, depth, half, ny), bf16),
                pltpu.VMEM((chips, bands, 2, depth, half, ny), bf16),
                pltpu.VMEM((chips, bands, 2, depth, half, ny), bf16),
                pltpu.VMEM((nx, nx), bf16),
                pltpu.VMEM((ny, ny), bf16),
                pltpu.VMEM((2, depth, nx, ny), f32),
                pltpu.VMEM((nb - 1, 2, depth, rows, ny), f32),
                pltpu.VMEM((nb, 3, depth, half, ny), f32),
                pltpu.VMEM((nb - 2, 3, depth, half, ny), f32),
                pltpu.VMEM((5, depth, half, ny), f32),
                dma,
                dma,
                dma((nb,)),
                dma((nb,)),
                dma((chips,)),
                dma((chips,)),
                dma((chips,)),
                dma((chips,)),
                dma((nb - 1,)),
                dma((nb - 1,)),
                dma((nb,)),
                dma((nb - 2,)),
                dma((2, 3)),
                dma((5,)),
                pltpu.SemaphoreType.REGULAR,
                pltpu.SemaphoreType.REGULAR,
            ],
            compiler_params=pltpu.CompilerParams(collective_id=0, has_side_effects=True, vmem_limit_bytes=55000 * 1024),
            name="current",
        )(occupations, orbitals)

    return jax.shard_map(
        per_device,
        mesh=mesh,
        in_specs=(P("band", None, "grid", None, None), P("band")),
        out_specs=P(None, "grid", "band", None),
        check_vma=False,
    )
```

time: 35.6 us -> 36.1 us (1.014)
  the two profiles are of different devices: /device:TPU:4 before, /device:TPU:0 now
where the time goes in v1:
time: 36.1 us; the launch traced here: 35.9 us
  Pallas kernels  34.6 us (96%)
  local copies, waits for them, and re-layouts  1.3 us (4%)
    pallas_call x1, Pallas kernels, per_device(): pl.pallas_call(functools.partial(kernel, nb, ng), out_shape=jax.ShapeDtyp...  34.6 us
    unnamed x3, local copies, waits for them, and re-layouts  1.3 us

profile of v1, /device:TPU:0, one launch (start us, length us, event | category | flops | bytes accessed | tf_op | source)
XLA Modules:
  0.0 35.9 jit_solution(10883002099935299276)
XLA Ops:
  0.0 0.0 copy-start
  0.0 0.7 %copy-done = f32[16]{0:T(128)S(1)} copy-done((f32[16]{0:T(128)S(1)}, f32[16]{0:T(128)}, u32[]{:S(2)}) %copy-start) | copy-done | bytes 88
  0.7 34.6 %current.1 = f32[3,2,32,128]{3,2,1,0:T(8,128)S(1)} custom-call(f32[16]{0:T(128)S(1)} %copy-done, bf16[16,2,2,128,128]{4,3,2,1,0:T(8,128)(2,1)} %orb_ref.1), custom_call_target="tpu_custom_call" | custom-call | tf_op jit(solution)/shard_map/current/pallas_call | solution.py:348
  35.3 0.6 %copy.4 = f32[3,2,32,128]{3,2,1,0:T(8,128)} copy(f32[3,2,32,128]{3,2,1,0:T(8,128)S(1)} %current.1) | data formatting | bytes 196608
Async XLA Ops:
  0.0 0.7 %copy-start = (f32[16]{0:T(128)S(1)}, f32[16]{0:T(128)}, u32[]{:S(2)}) copy-start(f32[16]{0:T(128)} %occ_hbm.1) | copy-start | bytes 196

commit v2 on v1

v2 whole, which is shorter than its diff:
```python
import functools

import jax
import jax.numpy as jnp
from jax import lax
from jax.experimental import pallas as pl
from jax.experimental.pallas import tpu as pltpu
from jax.sharding import PartitionSpec as P

TILE = 16
PAIRS = ((0, 1), (1, 2), (2, 3), (3, 4), (0, 2), (1, 3), (2, 4), (3, 5))


def stencil(n, flipped):
    row = lax.broadcasted_iota(jnp.int32, (n, n), 0)
    col = lax.broadcasted_iota(jnp.int32, (n, n), 1)
    d = col - row if flipped else row - col
    value = jnp.zeros((n, n), jnp.float32)
    for step, weight in ((1, 8.0), (-1, -8.0), (2, -1.0), (-2, 1.0)):
        hit = (d == step) | (d == step - n) | (d == step + n)
        value = jnp.where(hit, weight, value)
    return value.astype(jnp.bfloat16)


def kernel(
    nb, ng, occ_hbm, orb_ref, out_ref,
    occ_ref, own, mate, outer, inner, mx, my, plane_sum, plane_recv, zsend, inbox, final,
    occ_sem, own_sem, mate_send, mate_recv, outer_send, outer_recv, inner_send, inner_recv,
    plane_send_sem, plane_recv_sem, inbox_send, inbox_recv, final_send, last_send, final_recv, up_token, down_token,
):
    bands, _, depth, nx, ny = orb_ref.shape
    b = lax.axis_index("band")
    g = lax.axis_index("grid")
    odd = lax.rem(g, 2)
    turn = 1 - 2 * odd
    partner = g + turn
    ahead = lax.rem(g + 2 * turn + ng, ng)
    behind = lax.rem(g - 2 * turn + ng, ng)
    side = lax.rem(g - turn + ng, ng)
    layers = ng // 2
    layer = g // 2
    rows = nx // nb
    half = rows // 2
    chips = nb // 2
    chip = b // 2
    core = lax.rem(b, 2)
    split = bands // 2

    load = pltpu.make_async_copy(orb_ref, own, own_sem)
    load.start()
    weights = pltpu.make_async_copy(occ_hbm, occ_ref, occ_sem)
    weights.start()

    barrier = pltpu.get_barrier_semaphore()
    peers = [lax.rem(b + k, nb) for k in range(1, nb)]
    pl.semaphore_signal(barrier, inc=1, device_id={"band": b, "grid": partner})
    for peer in peers:
        pl.semaphore_signal(barrier, inc=1, device_id={"band": peer, "grid": g})

    @pl.when(layer > 0)
    def _():
        pl.semaphore_signal(barrier, inc=1, device_id={"band": b, "grid": g - 2})

    @pl.when(layer < layers - 1)
    def _():
        pl.semaphore_signal(barrier, inc=1, device_id={"band": b, "grid": g + 2})

    ends = (layer == 0).astype(jnp.int32) + (layer == layers - 1).astype(jnp.int32)
    pl.semaphore_wait(barrier, nb + 2 - ends)

    def chunk_of(j):
        return 2 * lax.rem(chip + 1 + j // 2, chips) + j % 2

    def rows_of(j, parity):
        return pl.ds(pl.multiple_of(chunk_of(j) * rows + parity * half, half), half)

    passed, straight = pl.ds(0, split), pl.ds(split, bands - split)

    def to_mate(j, kind):
        part = (passed, straight)[kind]
        return pltpu.make_async_remote_copy(
            src_ref=orb_ref.at[part, :, :, rows_of(j, 1 - odd), :],
            dst_ref=mate.at[j, part],
            send_sem=mate_send.at[kind, j],
            recv_sem=mate_recv.at[kind, j],
            device_id={"band": b, "grid": partner},
        )

    def to_outer(j, source):
        return pltpu.make_async_remote_copy(
            src_ref=source.at[straight, :, :, rows_of(j, odd), :],
            dst_ref=outer.at[j],
            send_sem=outer_send.at[j],
            recv_sem=outer_recv.at[j],
            device_id={"band": b, "grid": behind},
        )

    def to_inner(j):
        return pltpu.make_async_remote_copy(
            src_ref=mate.at[j, passed],
            dst_ref=inner.at[j],
            send_sem=inner_send.at[j],
            recv_sem=inner_recv.at[j],
            device_id={"band": b, "grid": ahead},
        )

    wraps = ((odd == 0) & (layer == 0)) | ((odd == 1) & (layer == layers - 1))
    for kind in (0, 1):
        for j in range(nb):
            to_mate(j, kind).start()

    @pl.when(jnp.logical_not(wraps))
    def _():
        for j in range(nb):
            to_outer(j, orb_ref).start()

    @pl.when(layer == 1)
    def _():
        pl.semaphore_signal(up_token, inc=1, device_id={"band": b, "grid": g + 2})

    @pl.when(layer == layers - 2)
    def _():
        pl.semaphore_signal(down_token, inc=1, device_id={"band": b, "grid": g - 2})

    @pl.when(layer >= 2)
    def _():
        pl.semaphore_wait(up_token, 1)

        @pl.when(layer < layers - 1)
        def _():
            pl.semaphore_signal(up_token, inc=1, device_id={"band": b, "grid": g + 2})

    @pl.when(layer <= layers - 3)
    def _():
        pl.semaphore_wait(down_token, 1)

        @pl.when(layer > 0)
        def _():
            pl.semaphore_signal(down_token, inc=1, device_id={"band": b, "grid": g - 2})

    load.wait()

    @pl.when(wraps)
    def _():
        for j in range(nb):
            to_outer(j, own).start()

    mx[...] = stencil(nx, True)
    my[...] = stencil(ny, False)
    plane_sum[...] = jnp.zeros_like(plane_sum)
    weights.wait()

    def lateral(n, carry):
        w = occ_ref[n]
        for s in range(depth):
            re = own[n, 0, s]
            im = own[n, 1, s]
            tx = jnp.dot(mx[...], jnp.concatenate([re, im], 1), preferred_element_type=jnp.float32)
            ty = jnp.dot(jnp.concatenate([re, im], 0), my[...], preferred_element_type=jnp.float32)
            wre = re.astype(jnp.float32) * w
            wim = im.astype(jnp.float32) * w
            plane_sum[0, s] += wre * tx[:, ny:] - wim * tx[:, :ny]
            plane_sum[1, s] += wre * ty[nx:] - wim * ty[:nx]
        return carry

    lax.fori_loop(0, bands, lateral, 0)

    def to_peer(k):
        peer = lax.rem(b + k, nb)
        return pltpu.make_async_remote_copy(
            src_ref=plane_sum.at[:, :, pl.ds(pl.multiple_of(peer * rows, rows), rows), :],
            dst_ref=plane_recv.at[k - 1],
            send_sem=plane_send_sem.at[k - 1],
            recv_sem=plane_recv_sem.at[k - 1],
            device_id={"band": peer, "grid": g},
        )

    for k in range(1, nb):
        to_peer(k).start()

    for j in range(nb):
        to_mate(j, 0).wait_recv()
        to_inner(j).start()

    mine = pl.ds(pl.multiple_of(b * rows, rows), rows)
    summed = plane_sum[:, :, mine, :]
    for k in range(1, nb):
        to_peer(k).wait_recv()
        summed = summed + plane_recv[k - 1]
    out_ref[1:3] = summed * (1.0 / 12.0)

    def depthwise(j, kind):
        first = odd if kind else 1 - odd
        second = 1 - first
        sign = (turn if kind else -turn).astype(jnp.float32)
        here = rows_of(j, odd)

        def at_home(n, q, p):
            return own[n, q, p, here, :].astype(jnp.float32)

        def at_mate(n, q, p):
            return mate[j, n, q, p].astype(jnp.float32)

        def at_far(n, q, p):
            return (outer[j, n - split, q, p] if kind else inner[j, n, q, p]).astype(jnp.float32)

        chain = (at_home, at_mate, at_far) if kind else (at_mate, at_home, at_far)

        def step(n, sums):
            w = occ_ref[n] * sign
            fields = [tuple(held(n, q, p) for q in (0, 1)) for held in chain for p in (first, second)]
            scaled = [(re * w, im * w) for re, im in fields[:4]]
            return tuple(
                total + (scaled[i][0] * fields[k][1] - scaled[i][1] * fields[k][0])
                for total, (i, k) in zip(sums, PAIRS)
            )

        zero = jnp.zeros((half, ny), jnp.float32)
        span = (split, bands) if kind else (0, split)
        n01, n12, n23, n34, f02, f13, f24, f35 = lax.fori_loop(*span, step, (zero,) * 8, unroll=4)
        parts = (
            (8.0 * n01 - f02, 8.0 * (n01 + n12) - f13),
            (8.0 * (n12 + n23) - f02 - f24, 8.0 * (n23 + n34) - f13 - f35),
            (8.0 * n34 - f24, -f35),
        )
        if kind:
            for role in range(3):
                zsend[j, role, first] = parts[role][0]
                zsend[j, role, second] = parts[role][1]
        else:
            for role in range(2):
                zsend[j, role, first] += parts[1 - role][0]
                zsend[j, role, second] += parts[1 - role][1]
            zsend[j, 3, first] = parts[2][0]
            zsend[j, 3, second] = parts[2][1]

    def to_inbox(j):
        chunk = chunk_of(j)
        slot = lax.rem(b - 2 * (chunk // 2) - 2 + nb, nb)
        return pltpu.make_async_remote_copy(
            src_ref=zsend.at[j],
            dst_ref=inbox.at[slot],
            send_sem=inbox_send.at[j],
            recv_sem=inbox_recv.at[slot],
            device_id={"band": chunk, "grid": g},
        )

    def from_inbox(slot):
        return pltpu.make_async_remote_copy(
            src_ref=zsend.at[0],
            dst_ref=inbox.at[slot],
            send_sem=inbox_send.at[0],
            recv_sem=inbox_recv.at[slot],
            device_id={"band": b, "grid": partner},
        )

    def to_final(j, role):
        slot = 2 * role - 1 + core if role else 0
        at = (g, partner, ahead, side)[role]
        return pltpu.make_async_remote_copy(
            src_ref=zsend.at[j, role],
            dst_ref=final.at[slot],
            send_sem=final_send.at[role],
            recv_sem=final_recv.at[slot],
            device_id={"band": 2 * chip + j % 2, "grid": at},
        )

    def to_last(role):
        slot = 2 * role - 1 + core if role else 0
        return pltpu.make_async_remote_copy(
            src_ref=zsend.at[nb - 1, role],
            dst_ref=final.at[slot],
            send_sem=last_send.at[role],
            recv_sem=final_recv.at[slot],
            device_id={"band": 2 * chip + 1, "grid": (g, partner, ahead, side)[role]},
        )

    def from_final(slot):
        return pltpu.make_async_remote_copy(
            src_ref=zsend.at[0, 0],
            dst_ref=final.at[slot],
            send_sem=final_send.at[0],
            recv_sem=final_recv.at[slot],
            device_id={"band": b, "grid": partner},
        )

    def straight_part(j):
        to_mate(j, 1).wait_recv()
        to_outer(j, orb_ref).wait_recv()
        depthwise(j, 1)

    def passed_part(j):
        to_inner(j).wait_recv()
        depthwise(j, 0)

    others = range(nb - 2)
    for j in range(nb - 2):
        straight_part(j)
        passed_part(j)
        to_inbox(j).start()

    straight_part(nb - 2)
    passed_part(nb - 2)

    @pl.when(core == 1)
    def _():
        to_inbox(nb - 2).start()

    @pl.when(core == 0)
    def _():
        for slot in (*others, nb - 1):
            from_inbox(slot).wait_recv()
        zsend[nb - 2] = zsend[nb - 2] + inbox[nb - 1] + sum(inbox[slot] for slot in others)
        for role in (2, 3, 1):
            to_final(nb - 2, role).start()

    straight_part(nb - 1)

    @pl.when(core == 1)
    def _():
        for slot in others:
            from_inbox(slot).wait_recv()
        zsend[nb - 1, :3] = zsend[nb - 1, :3] + sum(inbox[slot, :3] for slot in others)
        to_final(nb - 1, 2).start()

    @pl.when(core == 0)
    def _():
        to_last(2).start()

    passed_part(nb - 1)

    @pl.when(core == 1)
    def _():
        zsend[nb - 1, 3] = zsend[nb - 1, 3] + sum(inbox[slot, 3] for slot in others)
        for role in (3, 1):
            to_final(nb - 1, role).start()

    @pl.when(core == 0)
    def _():
        for role in (3, 1, 0):
            to_last(role).start()

    near = pl.ds(pl.multiple_of(odd * half, half), half)
    away = pl.ds(pl.multiple_of((1 - odd) * half, half), half)

    @pl.when(core == 1)
    def _():
        for slot in range(7):
            from_final(slot).wait_recv()
        out_ref[0, :, near, :] = (zsend[nb - 1, 0] + final[0] + final[3] + final[4]) * (1.0 / 12.0)
        out_ref[0, :, away, :] = (final[1] + final[2] + final[5] + final[6]) * (1.0 / 12.0)

    @pl.when(core == 0)
    def _():
        for slot in (1, 3, 5):
            from_final(slot).wait_recv()
        out_ref[0, :, near, :] = (zsend[nb - 2, 0] + final[3]) * (1.0 / 12.0)
        out_ref[0, :, away, :] = (final[1] + final[5]) * (1.0 / 12.0)

    for k in range(1, nb):
        to_peer(k).wait_send()
    for j in range(nb):
        to_mate(j, 0).wait_send()
        to_mate(j, 1).wait_send()
        to_outer(j, orb_ref).wait_send()
        to_inner(j).wait_send()
    for j in range(nb - 2):
        to_inbox(j).wait_send()

    @pl.when(core == 1)
    def _():
        to_inbox(nb - 2).wait_send()
        for role in (1, 2, 3):
            to_final(nb - 1, role).wait_send()

    @pl.when(core == 0)
    def _():
        for role in (1, 2, 3):
            to_final(nb - 2, role).wait_send()
        for role in range(4):
            to_last(role).wait_send()


def solution(mesh):
    nb = mesh.shape["band"]
    ng = mesh.shape["grid"]

    def per_device(orbitals, occupations):
        bands, _, depth, nx, ny = orbitals.shape
        rows = nx // nb
        half = rows // 2
        if depth != 2 or nb % 2 or nb < 4 or ng % 2 or ng < 6 or half % TILE:
            raise ValueError("unsupported sizes")
        f32, bf16 = jnp.float32, jnp.bfloat16
        dma = pltpu.SemaphoreType.DMA
        return pl.pallas_call(
            functools.partial(kernel, nb, ng),
            out_shape=jax.ShapeDtypeStruct((3, depth, rows, ny), f32),
            in_specs=[
                pl.BlockSpec(memory_space=pltpu.HBM),
                pl.BlockSpec(memory_space=pltpu.HBM),
            ],
            out_specs=pl.BlockSpec(memory_space=pltpu.VMEM),
            scratch_shapes=[
                pltpu.SMEM((bands,), f32),
                pltpu.VMEM((bands, 2, depth, nx, ny), bf16),
                pltpu.VMEM((nb, bands, 2, depth, half, ny), bf16),
                pltpu.VMEM((nb, bands - bands // 2, 2, depth, half, ny), bf16),
                pltpu.VMEM((nb, bands // 2, 2, depth, half, ny), bf16),
                pltpu.VMEM((nx, nx), bf16),
                pltpu.VMEM((ny, ny), bf16),
                pltpu.VMEM((2, depth, nx, ny), f32),
                pltpu.VMEM((nb - 1, 2, depth, rows, ny), f32),
                pltpu.VMEM((nb, 4, depth, half, ny), f32),
                pltpu.VMEM((nb, 4, depth, half, ny), f32),
                pltpu.VMEM((7, depth, half, ny), f32),
                dma,
                dma,
                dma((2, nb)),
                dma((2, nb)),
                dma((nb,)),
                dma((nb,)),
                dma((nb,)),
                dma((nb,)),
                dma((nb - 1,)),
                dma((nb - 1,)),
                dma((nb,)),
                dma((nb,)),
                dma((4,)),
                dma((4,)),
                dma((7,)),
                pltpu.SemaphoreType.REGULAR,
                pltpu.SemaphoreType.REGULAR,
            ],
            compiler_params=pltpu.CompilerParams(collective_id=0, has_side_effects=True, vmem_limit_bytes=55000 * 1024),
            name="current",
        )(pltpu.with_memory_space_constraint(occupations, pltpu.HBM), orbitals)

    return jax.shard_map(
        per_device,
        mesh=mesh,
        in_specs=(P("band", None, "grid", None, None), P("band")),
        out_specs=P(None, "grid", "band", None),
        check_vma=False,
    )
```

time: 36.1 us -> 34.7 us (0.961)
  the two profiles are of different devices: /device:TPU:0 before, /device:TPU:1 now
where the time goes in v2:
time: 34.7 us; the launch traced here: 34.5 us
  Pallas kernels  33.9 us (98%)
  local copies, waits for them, and re-layouts  0.64 us (2%)
    pallas_call x1, Pallas kernels, per_device(): pl.pallas_call(functools.partial(kernel, nb, ng), out_shape=jax.ShapeDtyp...  33.9 us

profile of v2, /device:TPU:1, one launch (start us, length us, event | category | flops | bytes accessed | tf_op | source)
XLA Modules:
  0.0 34.5 jit_solution(2989089805457110111)
XLA Ops:
  0.0 33.9 %current.1 = f32[3,2,32,128]{3,2,1,0:T(8,128)S(1)} custom-call(f32[16]{0:T(128)} %occ_hbm.1, bf16[16,2,2,128,128]{4,3,2,1,0:T(8,128)(2,1)} %orb_ref.1), custom_call_target="tpu_custom_call" | custom-call | tf_op jit(solution)/shard_map/current/pallas_call | solution.py:396
  33.9 0.6 %copy.4 = f32[3,2,32,128]{3,2,1,0:T(8,128)} copy(f32[3,2,32,128]{3,2,1,0:T(8,128)S(1)} %current.1) | data formatting | bytes 196608

commit v3 on v2

v3 whole, which is shorter than its diff:
```python
import functools

import jax
import jax.numpy as jnp
from jax import lax
from jax.experimental import pallas as pl
from jax.experimental.pallas import tpu as pltpu
from jax.sharding import PartitionSpec as P

TILE = 16
MIXED = ()
HELD = 0


def stencil(n, flipped):
    row = lax.broadcasted_iota(jnp.int32, (n, n), 0)
    col = lax.broadcasted_iota(jnp.int32, (n, n), 1)
    d = col - row if flipped else row - col
    value = jnp.zeros((n, n), jnp.float32)
    for step, weight in ((1, 8.0), (-1, -8.0), (2, -1.0), (-2, 1.0)):
        hit = (d == step) | (d == step - n) | (d == step + n)
        value = jnp.where(hit, weight, value)
    return value.astype(jnp.bfloat16)


def kernel(
    nb, ng, occ_hbm, orb_ref, out_ref,
    occ_ref, own, mate, outer, inner, mx, my, plane_sum, plane_recv, zsend, inbox, final,
    occ_sem, own_sem, mate_send, mate_recv, outer_send, outer_recv, inner_send, inner_recv,
    plane_send_sem, plane_recv_sem, inbox_send, inbox_recv, final_send, final_recv, up_token, down_token,
):
    bands, _, depth, nx, ny = orb_ref.shape
    b = lax.axis_index("band")
    g = lax.axis_index("grid")
    odd = lax.rem(g, 2)
    turn = 1 - 2 * odd
    partner = g + turn
    ahead = lax.rem(g + 2 * turn + ng, ng)
    behind = lax.rem(g - 2 * turn + ng, ng)
    side = lax.rem(g - turn + ng, ng)
    layers = ng // 2
    layer = g // 2
    rows = nx // nb
    half = rows // 2
    split = bands // 2
    relayed = nb // 2

    load = pltpu.make_async_copy(orb_ref, own, own_sem)
    load.start()
    weights = pltpu.make_async_copy(occ_hbm, occ_ref, occ_sem)
    weights.start()

    barrier = pltpu.get_barrier_semaphore()
    peers = [lax.rem(b + k, nb) for k in range(1, nb)]
    pl.semaphore_signal(barrier, inc=1, device_id={"band": b, "grid": partner})
    for peer in peers:
        pl.semaphore_signal(barrier, inc=1, device_id={"band": peer, "grid": g})

    @pl.when(layer > 0)
    def _():
        pl.semaphore_signal(barrier, inc=1, device_id={"band": b, "grid": g - 2})

    @pl.when(layer < layers - 1)
    def _():
        pl.semaphore_signal(barrier, inc=1, device_id={"band": b, "grid": g + 2})

    ends = (layer == 0).astype(jnp.int32) + (layer == layers - 1).astype(jnp.int32)
    pl.semaphore_wait(barrier, nb + 2 - ends)

    def rows_of(j, parity):
        return pl.ds(pl.multiple_of(j * rows + parity * half, half), half)

    passed, straight = pl.ds(0, split), pl.ds(split, bands - split)
    mixed = [j for j in MIXED if j < nb]
    last_passed = [split - (j in mixed) for j in range(nb)]

    def to_mate(j, kind):
        part = (passed, straight)[kind]
        return pltpu.make_async_remote_copy(
            src_ref=orb_ref.at[part, :, :, rows_of(j, 1 - odd), :],
            dst_ref=mate.at[j, part],
            send_sem=mate_send.at[kind, j],
            recv_sem=mate_recv.at[kind, j],
            device_id={"band": b, "grid": partner},
        )

    def to_outer(j, source):
        return pltpu.make_async_remote_copy(
            src_ref=source.at[straight, :, :, rows_of(j, odd), :],
            dst_ref=outer.at[j, pl.ds(1, bands - split)],
            send_sem=outer_send.at[0, j],
            recv_sem=outer_recv.at[0, j],
            device_id={"band": b, "grid": behind},
        )

    def to_outer_mixed(j):
        return pltpu.make_async_remote_copy(
            src_ref=orb_ref.at[split - 1, :, :, rows_of(j, odd), :],
            dst_ref=outer.at[j, 0],
            send_sem=outer_send.at[1, j],
            recv_sem=outer_recv.at[1, j],
            device_id={"band": b, "grid": behind},
        )

    def to_inner(j):
        return pltpu.make_async_remote_copy(
            src_ref=mate.at[j, pl.ds(0, last_passed[j])],
            dst_ref=inner.at[j, pl.ds(0, last_passed[j])],
            send_sem=inner_send.at[0, j],
            recv_sem=inner_recv.at[0, j],
            device_id={"band": b, "grid": ahead},
        )

    def to_inner_mixed(j):
        return pltpu.make_async_remote_copy(
            src_ref=mate.at[j, split - 1],
            dst_ref=inner.at[j, split - 1],
            send_sem=inner_send.at[1, j],
            recv_sem=inner_recv.at[1, j],
            device_id={"band": b, "grid": ahead},
        )

    wraps = ((odd == 0) & (layer == 0)) | ((odd == 1) & (layer == layers - 1))
    wraps_ahead = ((odd == 0) & (layer == layers - 1)) | ((odd == 1) & (layer == 0))
    for kind in (0, 1):
        for j in range(nb):
            to_mate(j, kind).start()

    @pl.when(jnp.logical_not(wraps))
    def _():
        for j in range(nb - HELD):
            to_outer(j, orb_ref).start()
        for j in mixed:
            to_outer_mixed(j).start()

    @pl.when(layer == 1)
    def _():
        pl.semaphore_signal(up_token, inc=1, device_id={"band": b, "grid": g + 2})

    @pl.when(layer == layers - 2)
    def _():
        pl.semaphore_signal(down_token, inc=1, device_id={"band": b, "grid": g - 2})

    @pl.when(layer >= 2)
    def _():
        pl.semaphore_wait(up_token, 1)

        @pl.when(layer < layers - 1)
        def _():
            pl.semaphore_signal(up_token, inc=1, device_id={"band": b, "grid": g + 2})

    @pl.when(layer <= layers - 3)
    def _():
        pl.semaphore_wait(down_token, 1)

        @pl.when(layer > 0)
        def _():
            pl.semaphore_signal(down_token, inc=1, device_id={"band": b, "grid": g - 2})

    load.wait()

    @pl.when(wraps)
    def _():
        for j in range(nb):
            to_outer(j, own).start()

    mx[...] = stencil(nx, True)
    my[...] = stencil(ny, False)
    plane_sum[...] = jnp.zeros_like(plane_sum)
    weights.wait()

    def lateral(n, carry):
        w = occ_ref[n]
        for s in range(depth):
            re = own[n, 0, s]
            im = own[n, 1, s]
            tx = jnp.dot(mx[...], jnp.concatenate([re, im], 1), preferred_element_type=jnp.float32)
            ty = jnp.dot(jnp.concatenate([re, im], 0), my[...], preferred_element_type=jnp.float32)
            wre = re.astype(jnp.float32) * w
            wim = im.astype(jnp.float32) * w
            plane_sum[0, s] += wre * tx[:, ny:] - wim * tx[:, :ny]
            plane_sum[1, s] += wre * ty[nx:] - wim * ty[:nx]
        return carry

    lax.fori_loop(0, bands, lateral, 0)

    def to_peer(k):
        peer = lax.rem(b + k, nb)
        return pltpu.make_async_remote_copy(
            src_ref=plane_sum.at[:, :, pl.ds(pl.multiple_of(peer * rows, rows), rows), :],
            dst_ref=plane_recv.at[k - 1],
            send_sem=plane_send_sem.at[k - 1],
            recv_sem=plane_recv_sem.at[k - 1],
            device_id={"band": peer, "grid": g},
        )

    for k in range(1, nb):
        to_peer(k).start()

    for j in range(nb):
        to_mate(j, 0).wait_recv()
        to_inner(j).start()
        if j in mixed:
            @pl.when(wraps_ahead)
            def _():
                to_inner_mixed(j).start()

    @pl.when(jnp.logical_not(wraps))
    def _():
        for j in range(nb - HELD, nb):
            to_outer(j, own).start()

    mine = pl.ds(pl.multiple_of(b * rows, rows), rows)
    summed = plane_sum[:, :, mine, :]
    for k in range(1, nb):
        to_peer(k).wait_recv()
        summed = summed + plane_recv[k - 1]
    out_ref[1:3] = summed * (1.0 / 12.0)

    first = odd
    second = 1 - odd
    sign = turn.astype(jnp.float32)
    zero = jnp.zeros((half, ny), jnp.float32)

    def fields_of(held, n):
        return [tuple(held(n, q, p) for q in (0, 1)) for p in (first, second)]

    def bonds(n, low, high, sums):
        w = occ_ref[n] * sign
        low = [(re * w, im * w) for re, im in low]
        pairs = ((1, 0), (0, 0), (1, 1))
        return tuple(
            total + (low[i][0] * high[k][1] - low[i][1] * high[k][0]) for total, (i, k) in zip(sums, pairs)
        )

    def at_home(j):
        return lambda n, q, p: own[n, q, p, rows_of(j, odd), :].astype(jnp.float32)

    def at_mate(j):
        return lambda n, q, p: mate[j, n, q, p].astype(jnp.float32)

    def core_part(j):
        def step(n, sums):
            low, high = fields_of(at_home(j), n), fields_of(at_mate(j), n)
            w = occ_ref[n] * sign
            inside = tuple(
                total + (slab[0][0] * w * slab[1][1] - slab[0][1] * w * slab[1][0])
                for total, slab in zip(sums[3:], (low, high))
            )
            return bonds(n, low, high, sums[:3]) + inside

        n12, f02, f13, n01, n23 = lax.fori_loop(0, bands, step, (zero,) * 5, unroll=4)
        zsend[j, 0, first] = 8.0 * n01 - f02
        zsend[j, 0, second] = 8.0 * (n01 + n12) - f13
        zsend[j, 1, first] = 8.0 * (n12 + n23) - f02
        zsend[j, 1, second] = 8.0 * n23 - f13

    def straight_part(j):
        def step(n, sums):
            far = fields_of(lambda n, q, p: outer[j, n - split + 1, q, p].astype(jnp.float32), n)
            return bonds(n, fields_of(at_mate(j), n), far, sums)

        sums = lax.fori_loop(split, bands, step, (zero,) * 3, unroll=True)
        if j in mixed:
            sums = lax.fori_loop(split - jnp.where(wraps_ahead, 0, 1), split, step, sums)
        n34, f24, f35 = sums
        zsend[j, 1, first] += -f24
        zsend[j, 1, second] += 8.0 * n34 - f35
        zsend[j, 2, first] = 8.0 * n34 - f24
        zsend[j, 2, second] = -f35

    def passed_part(j):
        def step(n, sums):
            far = fields_of(lambda n, q, p: inner[j, n, q, p].astype(jnp.float32), n)
            return bonds(n, far, fields_of(at_home(j), n), sums)

        sums = lax.fori_loop(0, last_passed[j], step, (zero,) * 3, unroll=True)
        if j in mixed:
            sums = lax.fori_loop(split - jnp.where(wraps, 1, 0), split, step, sums)
        n10, f20, f11 = sums
        zsend[j, 0, first] += 8.0 * n10 - f20
        zsend[j, 0, second] += -f11
        zsend[j, 3, first] = -f20
        zsend[j, 3, second] = 8.0 * n10 - f11

    def to_inbox(j):
        slot = lax.rem(b - j - 1 + nb, nb)
        return pltpu.make_async_remote_copy(
            src_ref=zsend.at[j],
            dst_ref=inbox.at[slot],
            send_sem=inbox_send.at[j],
            recv_sem=inbox_recv.at[slot],
            device_id={"band": j, "grid": g},
        )

    def from_inbox(slot):
        return pltpu.make_async_remote_copy(
            src_ref=zsend.at[0],
            dst_ref=inbox.at[slot],
            send_sem=inbox_send.at[0],
            recv_sem=inbox_recv.at[slot],
            device_id={"band": b, "grid": partner},
        )

    def to_final(j, role):
        return pltpu.make_async_remote_copy(
            src_ref=zsend.at[j, role],
            dst_ref=final.at[role, b],
            send_sem=final_send.at[j, role],
            recv_sem=final_recv.at[role, b],
            device_id={"band": j, "grid": (g, partner, ahead, side)[role]},
        )

    def from_final(role, source):
        return pltpu.make_async_remote_copy(
            src_ref=zsend.at[0, 0],
            dst_ref=final.at[role, source],
            send_sem=final_send.at[0, 0],
            recv_sem=final_recv.at[role, source],
            device_id={"band": b, "grid": partner},
        )

    def arrive_mate(j):
        to_mate(j, 1).wait_recv()

    def arrive_outer(j):
        to_outer(j, own).wait_recv()
        if j in mixed:
            @pl.when(jnp.logical_not(wraps_ahead))
            def _():
                to_outer_mixed(j).wait_recv()

    def arrive_inner(j):
        to_inner(j).wait_recv()
        if j in mixed:
            @pl.when(wraps)
            def _():
                to_inner_mixed(j).wait_recv()

    def finish(j):
        @pl.when(b == j)
        def _():
            for slot in range(nb - 1):
                from_inbox(slot).wait_recv()
            zsend[j] = zsend[j] + sum(inbox[slot] for slot in range(nb - 1))
            for role in (3, 2, 1):
                to_final(j, role).start()

    for j in range(relayed):
        arrive_mate(j)
        core_part(j)
        arrive_outer(j)
        straight_part(j)
        arrive_inner(j)
        passed_part(j)

        @pl.when(b != j)
        def _():
            to_inbox(j).start()

        if j:
            finish(j - 1)

    def straight_last(j, mate_too):
        arrive_outer(j)
        straight_part(j)
        to_final(j, 2).start()
        if mate_too:
            to_final(j, 1).start()

    def passed_last(j):
        arrive_inner(j)
        passed_part(j)
        to_final(j, 3).start()

        @pl.when(b != j)
        def _():
            to_final(j, 0).start()

    for j in range(relayed, nb - 1):
        arrive_mate(j)
        if j > relayed:
            to_final(j - 1, 1).start()
        core_part(j)
        straight_last(j, False)
        if j == relayed:
            finish(relayed - 1)
        passed_last(j)

    arrive_mate(nb - 1)
    to_final(nb - 2, 1).start()
    core_part(nb - 1)

    @pl.when(wraps_ahead)
    def _():
        straight_last(nb - 1, True)

    passed_last(nb - 1)

    @pl.when(jnp.logical_not(wraps_ahead))
    def _():
        straight_last(nb - 1, True)

    near = pl.ds(pl.multiple_of(odd * half, half), half)
    away = pl.ds(pl.multiple_of((1 - odd) * half, half), half)

    @pl.when(b >= relayed)
    def _():
        for role in (0, 2, 1, 3):
            for k in range(1 if role == 0 else 0, nb):
                from_final(role, lax.rem(b + k, nb)).wait_recv()
        home = zsend[b, 0] + sum(final[0, lax.rem(b + k, nb)] for k in range(1, nb))
        out_ref[0, :, near, :] = (home + sum(final[2, k] for k in range(nb))) * (1.0 / 12.0)
        out_ref[0, :, away, :] = sum(final[1, k] + final[3, k] for k in range(nb)) * (1.0 / 12.0)

    @pl.when(b < relayed)
    def _():
        for role in (2, 1, 3):
            from_final(role, b).wait_recv()
        out_ref[0, :, near, :] = (zsend[b, 0] + final[2, b]) * (1.0 / 12.0)
        out_ref[0, :, away, :] = (final[1, b] + final[3, b]) * (1.0 / 12.0)

    for k in range(1, nb):
        to_peer(k).wait_send()
    for j in range(nb):
        to_mate(j, 0).wait_send()
        to_mate(j, 1).wait_send()
        to_outer(j, own).wait_send()
        to_inner(j).wait_send()
    for j in mixed:
        @pl.when(jnp.logical_not(wraps))
        def _():
            to_outer_mixed(j).wait_send()

        @pl.when(wraps_ahead)
        def _():
            to_inner_mixed(j).wait_send()

    for j in range(nb):
        if j < relayed:
            @pl.when(b != j)
            def _():
                to_inbox(j).wait_send()

            @pl.when(b == j)
            def _():
                for role in (1, 2, 3):
                    to_final(j, role).wait_send()
        else:
            for role in (1, 2, 3):
                to_final(j, role).wait_send()

            @pl.when(b != j)
            def _():
                to_final(j, 0).wait_send()


def solution(mesh):
    nb = mesh.shape["band"]
    ng = mesh.shape["grid"]

    def per_device(orbitals, occupations):
        bands, _, depth, nx, ny = orbitals.shape
        rows = nx // nb
        half = rows // 2
        if depth != 2 or nb % 2 or nb < 4 or ng % 2 or ng < 6 or half % TILE:
            raise ValueError("unsupported sizes")
        f32, bf16 = jnp.float32, jnp.bfloat16
        dma = pltpu.SemaphoreType.DMA
        return pl.pallas_call(
            functools.partial(kernel, nb, ng),
            out_shape=jax.ShapeDtypeStruct((3, depth, rows, ny), f32),
            in_specs=[
                pl.BlockSpec(memory_space=pltpu.HBM),
                pl.BlockSpec(memory_space=pltpu.HBM),
            ],
            out_specs=pl.BlockSpec(memory_space=pltpu.VMEM),
            scratch_shapes=[
                pltpu.SMEM((bands,), f32),
                pltpu.VMEM((bands, 2, depth, nx, ny), bf16),
                pltpu.VMEM((nb, bands, 2, depth, half, ny), bf16),
                pltpu.VMEM((nb, bands - bands // 2 + 1, 2, depth, half, ny), bf16),
                pltpu.VMEM((nb, bands // 2, 2, depth, half, ny), bf16),
                pltpu.VMEM((nx, nx), bf16),
                pltpu.VMEM((ny, ny), bf16),
                pltpu.VMEM((2, depth, nx, ny), f32),
                pltpu.VMEM((nb - 1, 2, depth, rows, ny), f32),
                pltpu.VMEM((nb, 4, depth, half, ny), f32),
                pltpu.VMEM((nb - 1, 4, depth, half, ny), f32),
                pltpu.VMEM((4, nb, depth, half, ny), f32),
                dma,
                dma,
                dma((2, nb)),
                dma((2, nb)),
                dma((2, nb)),
                dma((2, nb)),
                dma((2, nb)),
                dma((2, nb)),
                dma((nb - 1,)),
                dma((nb - 1,)),
                dma((nb - 1,)),
                dma((nb - 1,)),
                dma((nb, 4)),
                dma((4, nb)),
                pltpu.SemaphoreType.REGULAR,
                pltpu.SemaphoreType.REGULAR,
            ],
            compiler_params=pltpu.CompilerParams(collective_id=0, has_side_effects=True, vmem_limit_bytes=55000 * 1024),
            name="current",
        )(pltpu.with_memory_space_constraint(occupations, pltpu.HBM), orbitals)

    return jax.shard_map(
        per_device,
        mesh=mesh,
        in_specs=(P("band", None, "grid", None, None), P("band")),
        out_specs=P(None, "grid", "band", None),
        check_vma=False,
    )
```

time: 34.7 us -> 34 us (0.980)
  the two profiles are of different devices: /device:TPU:1 before, /device:TPU:5 now
where the time goes in v3:
time: 34 us; the launch traced here: 33.9 us
  Pallas kernels  33.2 us (98%)
  local copies, waits for them, and re-layouts  0.64 us (2%)
    pallas_call x1, Pallas kernels, per_device(): pl.pallas_call(functools.partial(kernel, nb, ng), out_shape=jax.ShapeDtyp...  33.2 us

profile of v3, /device:TPU:5, one launch (start us, length us, event | category | flops | bytes accessed | tf_op | source)
XLA Modules:
  0.0 33.9 jit_solution(14417625360115061707)
XLA Ops:
  0.0 33.2 %current.1 = f32[3,2,32,128]{3,2,1,0:T(8,128)S(1)} custom-call(f32[16]{0:T(128)} %occ_hbm.1, bf16[16,2,2,128,128]{4,3,2,1,0:T(8,128)(2,1)} %orb_ref.1), custom_call_target="tpu_custom_call" | custom-call | tf_op jit(solution)/shard_map/current/pallas_call | solution.py:470
  33.2 0.6 %copy.4 = f32[3,2,32,128]{3,2,1,0:T(8,128)} copy(f32[3,2,32,128]{3,2,1,0:T(8,128)S(1)} %current.1) | data formatting | bytes 196608

commit v4 on v3

v4 whole, which is shorter than its diff:
```python
import functools

import jax
import jax.numpy as jnp
from jax import lax
from jax.experimental import pallas as pl
from jax.experimental.pallas import tpu as pltpu
from jax.sharding import PartitionSpec as P

TILE = 16
MIXED = (0,)
HELD = 1


def stencil(n, flipped):
    row = lax.broadcasted_iota(jnp.int32, (n, n), 0)
    col = lax.broadcasted_iota(jnp.int32, (n, n), 1)
    d = col - row if flipped else row - col
    value = jnp.zeros((n, n), jnp.float32)
    for step, weight in ((1, 8.0), (-1, -8.0), (2, -1.0), (-2, 1.0)):
        hit = (d == step) | (d == step - n) | (d == step + n)
        value = jnp.where(hit, weight, value)
    return value.astype(jnp.bfloat16)


def kernel(
    nb, ng, occ_hbm, orb_ref, out_ref,
    occ_ref, own, mate, outer, inner, mx, my, plane_sum, plane_recv, zsend, inbox, final,
    occ_sem, own_sem, mate_send, mate_recv, outer_send, outer_recv, inner_send, inner_recv,
    plane_send_sem, plane_recv_sem, inbox_send, inbox_recv, final_send, final_recv, partner_in, next_in, wrap_in, peers_in,
):
    bands, _, depth, nx, ny = orb_ref.shape
    b = lax.axis_index("band")
    g = lax.axis_index("grid")
    odd = lax.rem(g, 2)
    turn = 1 - 2 * odd
    partner = g + turn
    ahead = lax.rem(g + 2 * turn + ng, ng)
    behind = lax.rem(g - 2 * turn + ng, ng)
    side = lax.rem(g - turn + ng, ng)
    layers = ng // 2
    layer = g // 2
    rows = nx // nb
    half = rows // 2
    split = bands // 2
    relayed = nb // 2

    load = pltpu.make_async_copy(orb_ref, own, own_sem)
    load.start()
    weights = pltpu.make_async_copy(occ_hbm, occ_ref, occ_sem)
    weights.start()

    barrier = pltpu.get_barrier_semaphore()
    last = layers - 1

    def tell(semaphore, band, grid):
        pl.semaphore_signal(semaphore, inc=1, device_id={"band": band, "grid": grid})

    @pl.when(odd == 0)
    def _():
        tell(barrier, b, partner)

    @pl.when(layer < last)
    def _():
        tell(barrier, b, g + 2)

    @pl.when(layer == 0)
    def _():
        tell(barrier, b, g + 2 * last)

    chip = b // 2
    tell(barrier, b + 1 - 2 * lax.rem(b, 2), g)
    for k in range(2, nb):
        @pl.when(2 * chip + k < nb)
        def _():
            tell(barrier, 2 * chip + k, g)

    earlier = odd + (layer > 0).astype(jnp.int32) + (layer == last).astype(jnp.int32) + 2 * chip + 1
    pl.semaphore_wait(barrier, earlier)

    @pl.when(odd == 1)
    def _():
        tell(partner_in, b, partner)

    @pl.when(layer > 0)
    def _():
        tell(next_in, b, g - 2)

    @pl.when(layer == last)
    def _():
        tell(wrap_in, b, g - 2 * last)

    for k in range(1, nb - 1):
        @pl.when(2 * chip - k >= 0)
        def _():
            tell(peers_in, 2 * chip - k, g)

    def rows_of(j, parity):
        return pl.ds(pl.multiple_of(j * rows + parity * half, half), half)

    passed, straight = pl.ds(0, split), pl.ds(split, bands - split)
    mixed = [j for j in MIXED if j < nb]
    last_passed = [split - (j in mixed) for j in range(nb)]

    def to_mate(j, kind, source=None):
        source = own if source is None else source
        part = (passed, straight)[kind]
        return pltpu.make_async_remote_copy(
            src_ref=source.at[part, :, :, rows_of(j, 1 - odd), :],
            dst_ref=mate.at[j, part],
            send_sem=mate_send.at[kind, j],
            recv_sem=mate_recv.at[kind, j],
            device_id={"band": b, "grid": partner},
        )

    def to_outer(j, start, source=None):
        source = own if source is None else source
        part = pl.ds(start, bands - start)
        return pltpu.make_async_remote_copy(
            src_ref=source.at[part, :, :, rows_of(j, odd), :],
            dst_ref=outer.at[j, pl.ds(start - split + 1, bands - start)],
            send_sem=outer_send.at[j],
            recv_sem=outer_recv.at[j],
            device_id={"band": b, "grid": behind},
        )

    def to_inner(j, stop):
        return pltpu.make_async_remote_copy(
            src_ref=mate.at[j, pl.ds(0, stop)],
            dst_ref=inner.at[j, pl.ds(0, stop)],
            send_sem=inner_send.at[j],
            recv_sem=inner_recv.at[j],
            device_id={"band": b, "grid": ahead},
        )

    def by_wrap(wrapping, j, act):
        if j not in mixed:
            act(split)
            return

        @pl.when(wrapping)
        def _():
            act(split)

        @pl.when(jnp.logical_not(wrapping))
        def _():
            act(split - 1)

    wraps = ((odd == 0) & (layer == 0)) | ((odd == 1) & (layer == layers - 1))
    wraps_ahead = ((odd == 0) & (layer == layers - 1)) | ((odd == 1) & (layer == 0))
    plain_behind = wraps
    plain_ahead = wraps_ahead
    def start_mate(skip):
        for kind in (0, 1):
            for j in range(nb):
                if kind or j >= skip:
                    to_mate(j, kind).start()

    def start_outer(skip):
        for j in range(skip, nb - HELD):
            by_wrap(plain_behind, j, lambda start: to_outer(j, start).start())

        @pl.when(jnp.logical_not(wraps_ahead))
        def _():
            for j in range(nb - HELD, nb):
                by_wrap(plain_behind, j, lambda start: to_outer(j, start).start())

    known = ((odd == 0) & (layer > 0)) | ((odd == 1) & (layer == last))

    @pl.when(odd == 1)
    def _():
        to_mate(0, 0, orb_ref).start()

    @pl.when(known)
    def _():
        by_wrap(plain_behind, 0, lambda start: to_outer(0, start, orb_ref).start())

    load.wait()

    @pl.when(known)
    def _():
        start_outer(1)

    @pl.when(2 * chip + 2 < nb)
    def _():
        pl.semaphore_wait(peers_in, nb - 2 * chip - 2)

    @pl.when(odd == 1)
    def _():
        start_mate(1)

    @pl.when(odd == 0)
    def _():
        pl.semaphore_wait(partner_in, 1)
        start_mate(0)

    @pl.when(layer < last)
    def _():
        pl.semaphore_wait(next_in, 1)

    @pl.when((odd == 1) & (layer < last))
    def _():
        start_outer(0)

    @pl.when(layer == 0)
    def _():
        pl.semaphore_wait(wrap_in, 1)

    @pl.when((odd == 0) & (layer == 0))
    def _():
        start_outer(0)

    mx[...] = stencil(nx, True)
    my[...] = stencil(ny, False)
    plane_sum[...] = jnp.zeros_like(plane_sum)
    zsend[...] = jnp.zeros_like(zsend)
    weights.wait()

    def lateral(n, carry):
        w = occ_ref[n]
        for s in range(depth):
            re = own[n, 0, s]
            im = own[n, 1, s]
            tx = jnp.dot(mx[...], jnp.concatenate([re, im], 1), preferred_element_type=jnp.float32)
            ty = jnp.dot(jnp.concatenate([re, im], 0), my[...], preferred_element_type=jnp.float32)
            wre = re.astype(jnp.float32) * w
            wim = im.astype(jnp.float32) * w
            plane_sum[0, s] += wre * tx[:, ny:] - wim * tx[:, :ny]
            plane_sum[1, s] += wre * ty[nx:] - wim * ty[:nx]
        return carry

    lax.fori_loop(0, bands, lateral, 0)

    def to_peer(k):
        peer = lax.rem(b + k, nb)
        return pltpu.make_async_remote_copy(
            src_ref=plane_sum.at[:, :, pl.ds(pl.multiple_of(peer * rows, rows), rows), :],
            dst_ref=plane_recv.at[k - 1],
            send_sem=plane_send_sem.at[k - 1],
            recv_sem=plane_recv_sem.at[k - 1],
            device_id={"band": peer, "grid": g},
        )

    for k in range(1, nb):
        to_peer(k).start()

    for j in range(nb):
        to_mate(j, 0).wait_recv()
        by_wrap(plain_ahead, j, lambda stop: to_inner(j, stop).start())

    @pl.when(wraps_ahead)
    def _():
        for j in range(nb - HELD, nb):
            by_wrap(plain_behind, j, lambda start: to_outer(j, start).start())

    mine = pl.ds(pl.multiple_of(b * rows, rows), rows)
    summed = plane_sum[:, :, mine, :]
    for k in range(1, nb):
        to_peer(k).wait_recv()
        summed = summed + plane_recv[k - 1]
    out_ref[1:3] = summed * (1.0 / 12.0)

    first = odd
    second = 1 - odd
    sign = turn.astype(jnp.float32)
    zero = jnp.zeros((half, ny), jnp.float32)

    def fields_of(held, n):
        return [tuple(held(n, q, p) for q in (0, 1)) for p in (first, second)]

    def bonds(n, low, high, sums):
        w = occ_ref[n] * sign
        low = [(re * w, im * w) for re, im in low]
        pairs = ((1, 0), (0, 0), (1, 1))
        return tuple(
            total + (low[i][0] * high[k][1] - low[i][1] * high[k][0]) for total, (i, k) in zip(sums, pairs)
        )

    def at_home(j):
        return lambda n, q, p: own[n, q, p, rows_of(j, odd), :].astype(jnp.float32)

    def at_mate(j):
        return lambda n, q, p: mate[j, n, q, p].astype(jnp.float32)

    def core_part(j):
        def step(n, sums):
            low, high = fields_of(at_home(j), n), fields_of(at_mate(j), n)
            w = occ_ref[n] * sign
            inside = tuple(
                total + (slab[0][0] * w * slab[1][1] - slab[0][1] * w * slab[1][0])
                for total, slab in zip(sums[3:], (low, high))
            )
            return bonds(n, low, high, sums[:3]) + inside

        n12, f02, f13, n01, n23 = lax.fori_loop(0, bands, step, (zero,) * 5, unroll=4)
        zsend[j, 0, first] += 8.0 * n01 - f02
        zsend[j, 0, second] += 8.0 * (n01 + n12) - f13
        zsend[j, 2, first] += 8.0 * (n12 + n23) - f02
        zsend[j, 2, second] += 8.0 * n23 - f13

    def straight_part(j):
        def step(n, sums):
            far = fields_of(lambda n, q, p: outer[j, n - split + 1, q, p].astype(jnp.float32), n)
            return bonds(n, fields_of(at_mate(j), n), far, sums)

        sums = lax.fori_loop(split, bands, step, (zero,) * 3, unroll=True)
        if j in mixed:
            sums = lax.fori_loop(split - jnp.where(plain_ahead, 0, 1), split, step, sums)
        n34, f24, f35 = sums
        zsend[j, 2, first] += -f24
        zsend[j, 2, second] += 8.0 * n34 - f35
        zsend[j, 3, first] = 8.0 * n34 - f24
        zsend[j, 3, second] = -f35

    def passed_part(j):
        def step(n, sums):
            far = fields_of(lambda n, q, p: inner[j, n, q, p].astype(jnp.float32), n)
            return bonds(n, far, fields_of(at_home(j), n), sums)

        sums = lax.fori_loop(0, last_passed[j], step, (zero,) * 3, unroll=True)
        if j in mixed:
            sums = lax.fori_loop(split - jnp.where(plain_behind, 1, 0), split, step, sums)
        n10, f20, f11 = sums
        zsend[j, 0, first] += 8.0 * n10 - f20
        zsend[j, 0, second] += -f11
        zsend[j, 1, first] = -f20
        zsend[j, 1, second] = 8.0 * n10 - f11

    def to_inbox(j, kind):
        slot = lax.rem(b - j - 1 + nb, nb)
        return pltpu.make_async_remote_copy(
            src_ref=zsend.at[j, pl.ds(2 * kind, 2)],
            dst_ref=inbox.at[slot, pl.ds(2 * kind, 2)],
            send_sem=inbox_send.at[kind, j],
            recv_sem=inbox_recv.at[kind, slot],
            device_id={"band": j, "grid": g},
        )

    def from_inbox(slot, kind):
        return pltpu.make_async_remote_copy(
            src_ref=zsend.at[0, pl.ds(2 * kind, 2)],
            dst_ref=inbox.at[slot, pl.ds(2 * kind, 2)],
            send_sem=inbox_send.at[kind, 0],
            recv_sem=inbox_recv.at[kind, slot],
            device_id={"band": b, "grid": partner},
        )

    def to_final(j, role):
        return pltpu.make_async_remote_copy(
            src_ref=zsend.at[j, role],
            dst_ref=final.at[role, b],
            send_sem=final_send.at[j, role],
            recv_sem=final_recv.at[role, b],
            device_id={"band": j, "grid": (g, side, partner, ahead)[role]},
        )

    def from_final(role, source):
        return pltpu.make_async_remote_copy(
            src_ref=zsend.at[0, 0],
            dst_ref=final.at[role, source],
            send_sem=final_send.at[0, 0],
            recv_sem=final_recv.at[role, source],
            device_id={"band": b, "grid": partner},
        )

    def arrive_mate(j):
        to_mate(j, 1).wait_recv()

    def arrive_outer(j):
        by_wrap(plain_ahead, j, lambda start: to_outer(j, start).wait_recv())

    def arrive_inner(j):
        by_wrap(plain_behind, j, lambda stop: to_inner(j, stop).wait_recv())

    def finish(j):
        @pl.when(b == j)
        def _():
            for kind, roles in ((1, (3, 2)), (0, (1,))):
                pair = pl.ds(2 * kind, 2)
                for slot in range(nb - 1):
                    from_inbox(slot, kind).wait_recv()
                zsend[j, pair] = zsend[j, pair] + sum(inbox[slot, pair] for slot in range(nb - 1))
                for role in roles:
                    to_final(j, role).start()

    for j in range(relayed):
        arrive_mate(j)
        core_part(j)
        arrive_outer(j)
        straight_part(j)

        @pl.when(b != j)
        def _():
            to_inbox(j, 1).start()

        arrive_inner(j)
        passed_part(j)

        @pl.when(b != j)
        def _():
            to_inbox(j, 0).start()

        if j:
            finish(j - 1)

    def send_own(j):
        @pl.when(b != j)
        def _():
            to_final(j, 0).start()

    for j in range(relayed, nb - 1):
        arrive_mate(j)
        if j > relayed:
            to_final(j - 1, 2).start()
        core_part(j)
        arrive_outer(j)
        straight_part(j)
        to_final(j, 3).start()
        arrive_inner(j)
        passed_part(j)
        to_final(j, 1).start()
        send_own(j)

    end = nb - 1

    @pl.when(wraps)
    def _():
        arrive_inner(end)
        passed_part(end)
        to_final(end, 1).start()

    finish(relayed - 1)
    arrive_mate(end)
    to_final(end - 1, 2).start()

    @pl.when(wraps_ahead)
    def _():
        arrive_outer(end)
        straight_part(end)
        to_final(end, 3).start()

    core_part(end)

    @pl.when(wraps)
    def _():
        send_own(end)

    @pl.when(wraps_ahead)
    def _():
        to_final(end, 2).start()

    @pl.when(jnp.logical_not(wraps))
    def _():
        arrive_inner(end)
        passed_part(end)
        to_final(end, 1).start()
        send_own(end)

    @pl.when(jnp.logical_not(wraps_ahead))
    def _():
        arrive_outer(end)
        straight_part(end)
        to_final(end, 3).start()
        to_final(end, 2).start()

    near = pl.ds(pl.multiple_of(odd * half, half), half)
    away = pl.ds(pl.multiple_of((1 - odd) * half, half), half)

    @pl.when(b >= relayed)
    def _():
        for role in (0, 2, 3, 1):
            for k in range(1 if role == 0 else 0, nb):
                from_final(role, lax.rem(b + k, nb)).wait_recv()
        home = zsend[b, 0] + sum(final[0, lax.rem(b + k, nb)] for k in range(1, nb))
        out_ref[0, :, near, :] = (home + sum(final[3, k] for k in range(nb))) * (1.0 / 12.0)
        out_ref[0, :, away, :] = sum(final[2, k] + final[1, k] for k in range(nb)) * (1.0 / 12.0)

    @pl.when(b < relayed)
    def _():
        for role in (2, 3, 1):
            from_final(role, b).wait_recv()
        out_ref[0, :, near, :] = (zsend[b, 0] + final[3, b]) * (1.0 / 12.0)
        out_ref[0, :, away, :] = (final[2, b] + final[1, b]) * (1.0 / 12.0)

    for k in range(1, nb):
        to_peer(k).wait_send()
    for j in range(nb):
        to_mate(j, 0).wait_send()
        to_mate(j, 1).wait_send()
        by_wrap(plain_behind, j, lambda start: to_outer(j, start).wait_send())
        by_wrap(plain_ahead, j, lambda stop: to_inner(j, stop).wait_send())
    for j in range(nb):
        if j < relayed:
            @pl.when(b != j)
            def _():
                to_inbox(j, 0).wait_send()
                to_inbox(j, 1).wait_send()

            @pl.when(b == j)
            def _():
                for role in (1, 2, 3):
                    to_final(j, role).wait_send()
        else:
            for role in (1, 2, 3):
                to_final(j, role).wait_send()

            @pl.when(b != j)
            def _():
                to_final(j, 0).wait_send()


def solution(mesh):
    nb = mesh.shape["band"]
    ng = mesh.shape["grid"]

    def per_device(orbitals, occupations):
        bands, _, depth, nx, ny = orbitals.shape
        rows = nx // nb
        half = rows // 2
        if depth != 2 or nb % 2 or nb < 4 or ng % 2 or ng < 6 or half % TILE:
            raise ValueError("unsupported sizes")
        f32, bf16 = jnp.float32, jnp.bfloat16
        dma = pltpu.SemaphoreType.DMA
        return pl.pallas_call(
            functools.partial(kernel, nb, ng),
            out_shape=jax.ShapeDtypeStruct((3, depth, rows, ny), f32),
            in_specs=[
                pl.BlockSpec(memory_space=pltpu.HBM),
                pl.BlockSpec(memory_space=pltpu.HBM),
            ],
            out_specs=pl.BlockSpec(memory_space=pltpu.VMEM),
            scratch_shapes=[
                pltpu.SMEM((bands,), f32),
                pltpu.VMEM((bands, 2, depth, nx, ny), bf16),
                pltpu.VMEM((nb, bands, 2, depth, half, ny), bf16),
                pltpu.VMEM((nb, bands - bands // 2 + 1, 2, depth, half, ny), bf16),
                pltpu.VMEM((nb, bands // 2, 2, depth, half, ny), bf16),
                pltpu.VMEM((nx, nx), bf16),
                pltpu.VMEM((ny, ny), bf16),
                pltpu.VMEM((2, depth, nx, ny), f32),
                pltpu.VMEM((nb - 1, 2, depth, rows, ny), f32),
                pltpu.VMEM((nb, 4, depth, half, ny), f32),
                pltpu.VMEM((nb - 1, 4, depth, half, ny), f32),
                pltpu.VMEM((4, nb, depth, half, ny), f32),
                dma,
                dma,
                dma((2, nb)),
                dma((2, nb)),
                dma((nb,)),
                dma((nb,)),
                dma((nb,)),
                dma((nb,)),
                dma((nb - 1,)),
                dma((nb - 1,)),
                dma((2, nb - 1)),
                dma((2, nb - 1)),
                dma((nb, 4)),
                dma((4, nb)),
                pltpu.SemaphoreType.REGULAR,
                pltpu.SemaphoreType.REGULAR,
                pltpu.SemaphoreType.REGULAR,
                pltpu.SemaphoreType.REGULAR,
            ],
            compiler_params=pltpu.CompilerParams(collective_id=0, has_side_effects=True, vmem_limit_bytes=55000 * 1024),
            name="current",
        )(pltpu.with_memory_space_constraint(occupations, pltpu.HBM), orbitals)

    return jax.shard_map(
        per_device,
        mesh=mesh,
        in_specs=(P("band", None, "grid", None, None), P("band")),
        out_specs=P(None, "grid", "band", None),
        check_vma=False,
    )
```

time: 34 us -> 33.2 us (0.976)
  the two profiles are of different devices: /device:TPU:5 before, /device:TPU:1 now
where the time goes in v4:
time: 33.2 us; the launch traced here: 33.1 us
  Pallas kernels  32.4 us (98%)
  local copies, waits for them, and re-layouts  0.64 us (2%)
    pallas_call x1, Pallas kernels, per_device(): pl.pallas_call(functools.partial(kernel, nb, ng), out_shape=jax.ShapeDtyp...  32.4 us

profile of v4, /device:TPU:1, one launch (start us, length us, event | category | flops | bytes accessed | tf_op | source)
XLA Modules:
  0.0 33.1 jit_solution(9470628063105854991)
XLA Ops:
  0.0 32.4 %current.1 = f32[3,2,32,128]{3,2,1,0:T(8,128)S(1)} custom-call(f32[16]{0:T(128)} %occ_hbm.1, bf16[16,2,2,128,128]{4,3,2,1,0:T(8,128)(2,1)} %orb_ref.1), custom_call_target="tpu_custom_call" | custom-call | tf_op jit(solution)/shard_map/current/pallas_call | solution.py:524
  32.4 0.6 %copy.4 = f32[3,2,32,128]{3,2,1,0:T(8,128)} copy(f32[3,2,32,128]{3,2,1,0:T(8,128)S(1)} %current.1) | data formatting | bytes 196608

commit v5 on v4

--- a/solution.py
+++ b/solution.py
@@ -8,7 +8,7 @@
 from jax.sharding import PartitionSpec as P
 
 TILE = 16
-MIXED = (0,)
+MIXED = 1
 HELD = 1
 
 
@@ -95,11 +95,16 @@
         def _():
             tell(peers_in, 2 * chip - k, g)
 
+    def bytes_of(ref, semaphore):
+        return pltpu.make_async_remote_copy(
+            src_ref=ref, dst_ref=ref, send_sem=semaphore, recv_sem=semaphore, device_id={"band": b, "grid": partner}
+        )
+
     def rows_of(j, parity):
         return pl.ds(pl.multiple_of(j * rows + parity * half, half), half)
 
     passed, straight = pl.ds(0, split), pl.ds(split, bands - split)
-    mixed = [j for j in MIXED if j < nb]
+    mixed = range(MIXED)
     last_passed = [split - (j in mixed) for j in range(nb)]
 
     def to_mate(j, kind, source=None):
@@ -108,7 +113,7 @@
         return pltpu.make_async_remote_copy(
             src_ref=source.at[part, :, :, rows_of(j, 1 - odd), :],
             dst_ref=mate.at[j, part],
-            send_sem=mate_send.at[kind, j],
+            send_sem=mate_send,
             recv_sem=mate_recv.at[kind, j],
             device_id={"band": b, "grid": partner},
         )
@@ -119,7 +124,7 @@
         return pltpu.make_async_remote_copy(
             src_ref=source.at[part, :, :, rows_of(j, odd), :],
             dst_ref=outer.at[j, pl.ds(start - split + 1, bands - start)],
-            send_sem=outer_send.at[j],
+            send_sem=outer_send.at[int(j in mixed)],
             recv_sem=outer_recv.at[j],
             device_id={"band": b, "grid": behind},
         )
@@ -128,7 +133,7 @@
         return pltpu.make_async_remote_copy(
             src_ref=mate.at[j, pl.ds(0, stop)],
             dst_ref=inner.at[j, pl.ds(0, stop)],
-            send_sem=inner_send.at[j],
+            send_sem=inner_send.at[int(j in mixed)],
             recv_sem=inner_recv.at[j],
             device_id={"band": b, "grid": ahead},
         )
@@ -236,8 +241,8 @@
         return pltpu.make_async_remote_copy(
             src_ref=plane_sum.at[:, :, pl.ds(pl.multiple_of(peer * rows, rows), rows), :],
             dst_ref=plane_recv.at[k - 1],
-            send_sem=plane_send_sem.at[k - 1],
-            recv_sem=plane_recv_sem.at[k - 1],
+            send_sem=plane_send_sem,
+            recv_sem=plane_recv_sem,
             device_id={"band": peer, "grid": g},
         )
 
@@ -255,8 +260,8 @@
 
     mine = pl.ds(pl.multiple_of(b * rows, rows), rows)
     summed = plane_sum[:, :, mine, :]
+    bytes_of(plane_recv, plane_recv_sem).wait_recv()
     for k in range(1, nb):
-        to_peer(k).wait_recv()
         summed = summed + plane_recv[k - 1]
     out_ref[1:3] = summed * (1.0 / 12.0)
 
@@ -326,41 +331,23 @@
         zsend[j, 1, first] = -f20
         zsend[j, 1, second] = 8.0 * n10 - f11
 
-    def to_inbox(j, kind):
+    def to_inbox(j, role):
         slot = lax.rem(b - j - 1 + nb, nb)
         return pltpu.make_async_remote_copy(
-            src_ref=zsend.at[j, pl.ds(2 * kind, 2)],
-            dst_ref=inbox.at[slot, pl.ds(2 * kind, 2)],
-            send_sem=inbox_send.at[kind, j],
-            recv_sem=inbox_recv.at[kind, slot],
+            src_ref=zsend.at[j, role],
+            dst_ref=inbox.at[role, slot],
+            send_sem=inbox_send,
+            recv_sem=inbox_recv.at[role % 2 + role // 3],
             device_id={"band": j, "grid": g},
         )
 
-    def from_inbox(slot, kind):
-        return pltpu.make_async_remote_copy(
-            src_ref=zsend.at[0, pl.ds(2 * kind, 2)],
-            dst_ref=inbox.at[slot, pl.ds(2 * kind, 2)],
-            send_sem=inbox_send.at[kind, 0],
-            recv_sem=inbox_recv.at[kind, slot],
-            device_id={"band": b, "grid": partner},
-        )
-
     def to_final(j, role):
         return pltpu.make_async_remote_copy(
             src_ref=zsend.at[j, role],
-            dst_ref=final.at[role, b],
-            send_sem=final_send.at[j, role],
-            recv_sem=final_recv.at[role, b],
+            dst_ref=final.at[role * nb + b],
+            send_sem=final_send,
+            recv_sem=final_recv,
             device_id={"band": j, "grid": (g, side, partner, ahead)[role]},
-        )
-
-    def from_final(role, source):
-        return pltpu.make_async_remote_copy(
-            src_ref=zsend.at[0, 0],
-            dst_ref=final.at[role, source],
-            send_sem=final_send.at[0, 0],
-            recv_sem=final_recv.at[role, source],
-            device_id={"band": b, "grid": partner},
         )
 
     def arrive_mate(j):
@@ -375,13 +362,12 @@
     def finish(j):
         @pl.when(b == j)
         def _():
-            for kind, roles in ((1, (3, 2)), (0, (1,))):
-                pair = pl.ds(2 * kind, 2)
-                for slot in range(nb - 1):
-                    from_inbox(slot, kind).wait_recv()
-                zsend[j, pair] = zsend[j, pair] + sum(inbox[slot, pair] for slot in range(nb - 1))
+            for part, roles in ((2, (3,)), (1, (1,)), (0, (0, 2))):
+                bytes_of(inbox.at[pl.ds(0, len(roles))], inbox_recv.at[part]).wait_recv()
                 for role in roles:
-                    to_final(j, role).start()
+                    zsend[j, role] = zsend[j, role] + sum(inbox[role, slot] for slot in range(nb - 1))
+                    if role:
+                        to_final(j, role).start()
 
     for j in range(relayed):
         arrive_mate(j)
@@ -391,14 +377,15 @@
 
         @pl.when(b != j)
         def _():
-            to_inbox(j, 1).start()
+            to_inbox(j, 3).start()
 
         arrive_inner(j)
         passed_part(j)
 
         @pl.when(b != j)
         def _():
-            to_inbox(j, 0).start()
+            for role in (1, 2, 0):
+                to_inbox(j, role).start()
 
         if j:
             finish(j - 1)
@@ -468,45 +455,37 @@
 
     @pl.when(b >= relayed)
     def _():
-        for role in (0, 2, 3, 1):
-            for k in range(1 if role == 0 else 0, nb):
-                from_final(role, lax.rem(b + k, nb)).wait_recv()
-        home = zsend[b, 0] + sum(final[0, lax.rem(b + k, nb)] for k in range(1, nb))
-        out_ref[0, :, near, :] = (home + sum(final[3, k] for k in range(nb))) * (1.0 / 12.0)
-        out_ref[0, :, away, :] = sum(final[2, k] + final[1, k] for k in range(nb)) * (1.0 / 12.0)
+        bytes_of(final.at[pl.ds(0, 4 * nb - 1)], final_recv).wait_recv()
+        home = zsend[b, 0] + sum(final[lax.rem(b + k, nb)] for k in range(1, nb))
+        out_ref[0, :, near, :] = (home + sum(final[3 * nb + k] for k in range(nb))) * (1.0 / 12.0)
+        out_ref[0, :, away, :] = sum(final[2 * nb + k] + final[nb + k] for k in range(nb)) * (1.0 / 12.0)
 
     @pl.when(b < relayed)
     def _():
-        for role in (2, 3, 1):
-            from_final(role, b).wait_recv()
-        out_ref[0, :, near, :] = (zsend[b, 0] + final[3, b]) * (1.0 / 12.0)
-        out_ref[0, :, away, :] = (final[2, b] + final[1, b]) * (1.0 / 12.0)
-
-    for k in range(1, nb):
-        to_peer(k).wait_send()
-    for j in range(nb):
-        to_mate(j, 0).wait_send()
-        to_mate(j, 1).wait_send()
-        by_wrap(plain_behind, j, lambda start: to_outer(j, start).wait_send())
-        by_wrap(plain_ahead, j, lambda stop: to_inner(j, stop).wait_send())
-    for j in range(nb):
-        if j < relayed:
-            @pl.when(b != j)
-            def _():
-                to_inbox(j, 0).wait_send()
-                to_inbox(j, 1).wait_send()
-
-            @pl.when(b == j)
-            def _():
-                for role in (1, 2, 3):
-                    to_final(j, role).wait_send()
-        else:
-            for role in (1, 2, 3):
-                to_final(j, role).wait_send()
-
-            @pl.when(b != j)
-            def _():
-                to_final(j, 0).wait_send()
+        bytes_of(final.at[pl.ds(0, 3)], final_recv).wait_recv()
+        out_ref[0, :, near, :] = (zsend[b, 0] + final[3 * nb + b]) * (1.0 / 12.0)
+        out_ref[0, :, away, :] = (final[2 * nb + b] + final[nb + b]) * (1.0 / 12.0)
+
+    bytes_of(plane_recv, plane_send_sem).wait_send()
+    bytes_of(mate, mate_send).wait_send()
+    bytes_of(outer.at[pl.ds(MIXED, nb - MIXED), pl.ds(1, bands - split)], outer_send.at[0]).wait_send()
+    bytes_of(inner.at[pl.ds(MIXED, nb - MIXED)], inner_send.at[0]).wait_send()
+    if MIXED:
+        whole = pl.ds(0, MIXED)
+        by_wrap(plain_behind, 0, lambda start: bytes_of(
+            outer.at[whole, pl.ds(start - split + 1, bands - start)], outer_send.at[1]).wait_send())
+        by_wrap(plain_ahead, 0, lambda stop: bytes_of(inner.at[whole, pl.ds(0, stop)], inner_send.at[1]).wait_send())
+    direct = 4 * (nb - relayed)
+
+    @pl.when(b >= relayed)
+    def _():
+        bytes_of(zsend.at[pl.ds(0, relayed)], inbox_send).wait_send()
+        bytes_of(final.at[pl.ds(0, direct - 1)], final_send).wait_send()
+
+    @pl.when(b < relayed)
+    def _():
+        bytes_of(zsend.at[pl.ds(0, relayed - 1)], inbox_send).wait_send()
+        bytes_of(final.at[pl.ds(0, direct + 3)], final_send).wait_send()
 
 
 def solution(mesh):
@@ -540,22 +519,22 @@
                 pltpu.VMEM((2, depth, nx, ny), f32),
                 pltpu.VMEM((nb - 1, 2, depth, rows, ny), f32),
                 pltpu.VMEM((nb, 4, depth, half, ny), f32),
-                pltpu.VMEM((nb - 1, 4, depth, half, ny), f32),
-                pltpu.VMEM((4, nb, depth, half, ny), f32),
+                pltpu.VMEM((4, nb - 1, depth, half, ny), f32),
+                pltpu.VMEM((4 * nb, depth, half, ny), f32),
+                dma,
                 dma,
                 dma,
                 dma((2, nb)),
-                dma((2, nb)),
+                dma((2,)),
                 dma((nb,)),
+                dma((2,)),
                 dma((nb,)),
-                dma((nb,)),
-                dma((nb,)),
-                dma((nb - 1,)),
-                dma((nb - 1,)),
-                dma((2, nb - 1)),
-                dma((2, nb - 1)),
-                dma((nb, 4)),
-                dma((4, nb)),
+                dma,
+                dma,
+                dma,
+                dma((3,)),
+                dma,
+                dma,
                 pltpu.SemaphoreType.REGULAR,
                 pltpu.SemaphoreType.REGULAR,
                 pltpu.SemaphoreType.REGULAR,

time: 33.2 us -> 32.6 us (0.982); the launches traced: 33.1 us -> 32.1 us
  Pallas kernels: 32.4 us -> 31.4 us
    pallas_call x1, Pallas kernels: 32.4 us -> 31.4 us  [per_device(): pl.pallas_call(functools.partial(kernel, nb, ng), out_shape=jax.ShapeDtyp...]
where the time goes in v5:
time: 32.6 us; the launch traced here: 32.1 us
  Pallas kernels  31.4 us (96%)
  local copies, waits for them, and re-layouts  0.64 us (2%)
    pallas_call x1, Pallas kernels, per_device(): pl.pallas_call(functools.partial(kernel, nb, ng), out_shape=jax.ShapeDtyp...  31.4 us

profile of v5, /device:TPU:1, one launch (start us, length us, event | category | flops | bytes accessed | tf_op | source)
XLA Modules:
  0.0 32.1 jit_solution(6442085723508329867)
XLA Ops:
  0.0 31.4 %current.1 = f32[3,2,32,128]{3,2,1,0:T(8,128)S(1)} custom-call(f32[16]{0:T(128)} %occ_hbm.1, bf16[16,2,2,128,128]{4,3,2,1,0:T(8,128)(2,1)} %orb_ref.1), custom_call_target="tpu_custom_call" | custom-call | tf_op jit(solution)/shard_map/current/pallas_call | solution.py:503
  31.4 0.6 %copy.4 = f32[3,2,32,128]{3,2,1,0:T(8,128)} copy(f32[3,2,32,128]{3,2,1,0:T(8,128)S(1)} %current.1) | data formatting | bytes 196608

commit v6 on v5

--- a/solution.py
+++ b/solution.py
@@ -8,7 +8,7 @@
 from jax.sharding import PartitionSpec as P
 
 TILE = 16
-MIXED = 1
+MIXED = (3, 1)
 HELD = 1
 
 
@@ -25,9 +25,8 @@
 
 def kernel(
     nb, ng, occ_hbm, orb_ref, out_ref,
-    occ_ref, own, mate, outer, inner, mx, my, plane_sum, plane_recv, zsend, inbox, final,
-    occ_sem, own_sem, mate_send, mate_recv, outer_send, outer_recv, inner_send, inner_recv,
-    plane_send_sem, plane_recv_sem, inbox_send, inbox_recv, final_send, final_recv, partner_in, next_in, wrap_in, peers_in,
+    occ_ref, own, mate, outer, inner, mx, my, plane_sum, plane_recv, zsend, inbox, final, measure,
+    occ_sem, own_sem, sent, mate_recv, outer_recv, inner_recv, plane_recv_sem, inbox_recv, final_recv, answers, wrap_in,
 ):
     bands, _, depth, nx, ny = orb_ref.shape
     b = lax.axis_index("band")
@@ -80,11 +79,11 @@
 
     @pl.when(odd == 1)
     def _():
-        tell(partner_in, b, partner)
+        tell(answers, b, partner)
 
     @pl.when(layer > 0)
     def _():
-        tell(next_in, b, g - 2)
+        tell(answers, b, g - 2)
 
     @pl.when(layer == last)
     def _():
@@ -93,7 +92,7 @@
     for k in range(1, nb - 1):
         @pl.when(2 * chip - k >= 0)
         def _():
-            tell(peers_in, 2 * chip - k, g)
+            tell(answers, 2 * chip - k, g)
 
     def bytes_of(ref, semaphore):
         return pltpu.make_async_remote_copy(
@@ -104,8 +103,6 @@
         return pl.ds(pl.multiple_of(j * rows + parity * half, half), half)
 
     passed, straight = pl.ds(0, split), pl.ds(split, bands - split)
-    mixed = range(MIXED)
-    last_passed = [split - (j in mixed) for j in range(nb)]
 
     def to_mate(j, kind, source=None):
         source = own if source is None else source
@@ -113,7 +110,7 @@
         return pltpu.make_async_remote_copy(
             src_ref=source.at[part, :, :, rows_of(j, 1 - odd), :],
             dst_ref=mate.at[j, part],
-            send_sem=mate_send,
+            send_sem=sent,
             recv_sem=mate_recv.at[kind, j],
             device_id={"band": b, "grid": partner},
         )
@@ -124,7 +121,7 @@
         return pltpu.make_async_remote_copy(
             src_ref=source.at[part, :, :, rows_of(j, odd), :],
             dst_ref=outer.at[j, pl.ds(start - split + 1, bands - start)],
-            send_sem=outer_send.at[int(j in mixed)],
+            send_sem=sent,
             recv_sem=outer_recv.at[j],
             device_id={"band": b, "grid": behind},
         )
@@ -133,28 +130,34 @@
         return pltpu.make_async_remote_copy(
             src_ref=mate.at[j, pl.ds(0, stop)],
             dst_ref=inner.at[j, pl.ds(0, stop)],
-            send_sem=inner_send.at[int(j in mixed)],
+            send_sem=sent,
             recv_sem=inner_recv.at[j],
             device_id={"band": b, "grid": ahead},
         )
 
     def by_wrap(wrapping, j, act):
-        if j not in mixed:
+        if j >= max(MIXED):
             act(split)
             return
-
-        @pl.when(wrapping)
+        plain = wrapping
+        for parity in (0, 1):
+            if j >= MIXED[parity]:
+                plain = plain | (odd == parity)
+
+        @pl.when(plain)
         def _():
             act(split)
 
-        @pl.when(jnp.logical_not(wrapping))
+        @pl.when(jnp.logical_not(plain))
         def _():
             act(split - 1)
+
+    def shifted(wrapping, j):
+        by_parity = jnp.where(odd == 1, int(j < MIXED[1]), int(j < MIXED[0]))
+        return jnp.where(wrapping, 0, by_parity)
 
     wraps = ((odd == 0) & (layer == 0)) | ((odd == 1) & (layer == layers - 1))
     wraps_ahead = ((odd == 0) & (layer == layers - 1)) | ((odd == 1) & (layer == 0))
-    plain_behind = wraps
-    plain_ahead = wraps_ahead
     def start_mate(skip):
         for kind in (0, 1):
             for j in range(nb):
@@ -163,12 +166,12 @@
 
     def start_outer(skip):
         for j in range(skip, nb - HELD):
-            by_wrap(plain_behind, j, lambda start: to_outer(j, start).start())
+            by_wrap(wraps, j, lambda start: to_outer(j, start).start())
 
         @pl.when(jnp.logical_not(wraps_ahead))
         def _():
             for j in range(nb - HELD, nb):
-                by_wrap(plain_behind, j, lambda start: to_outer(j, start).start())
+                by_wrap(wraps, j, lambda start: to_outer(j, start).start())
 
     known = ((odd == 0) & (layer > 0)) | ((odd == 1) & (layer == last))
 
@@ -178,7 +181,7 @@
 
     @pl.when(known)
     def _():
-        by_wrap(plain_behind, 0, lambda start: to_outer(0, start, orb_ref).start())
+        by_wrap(wraps, 0, lambda start: to_outer(0, start, orb_ref).start())
 
     load.wait()
 
@@ -186,9 +189,11 @@
     def _():
         start_outer(1)
 
-    @pl.when(2 * chip + 2 < nb)
-    def _():
-        pl.semaphore_wait(peers_in, nb - 2 * chip - 2)
+    later = nb - 2 * chip - 2 + (1 - odd) + (layer < last).astype(jnp.int32)
+
+    @pl.when(later > 0)
+    def _():
+        pl.semaphore_wait(answers, later)
 
     @pl.when(odd == 1)
     def _():
@@ -196,12 +201,7 @@
 
     @pl.when(odd == 0)
     def _():
-        pl.semaphore_wait(partner_in, 1)
         start_mate(0)
-
-    @pl.when(layer < last)
-    def _():
-        pl.semaphore_wait(next_in, 1)
 
     @pl.when((odd == 1) & (layer < last))
     def _():
@@ -241,7 +241,7 @@
         return pltpu.make_async_remote_copy(
             src_ref=plane_sum.at[:, :, pl.ds(pl.multiple_of(peer * rows, rows), rows), :],
             dst_ref=plane_recv.at[k - 1],
-            send_sem=plane_send_sem,
+            send_sem=sent,
             recv_sem=plane_recv_sem,
             device_id={"band": peer, "grid": g},
         )
@@ -251,12 +251,12 @@
 
     for j in range(nb):
         to_mate(j, 0).wait_recv()
-        by_wrap(plain_ahead, j, lambda stop: to_inner(j, stop).start())
+        by_wrap(wraps_ahead, j, lambda stop: to_inner(j, stop).start())
 
     @pl.when(wraps_ahead)
     def _():
         for j in range(nb - HELD, nb):
-            by_wrap(plain_behind, j, lambda start: to_outer(j, start).start())
+            by_wrap(wraps, j, lambda start: to_outer(j, start).start())
 
     mine = pl.ds(pl.multiple_of(b * rows, rows), rows)
     summed = plane_sum[:, :, mine, :]
@@ -309,8 +309,8 @@
             return bonds(n, fields_of(at_mate(j), n), far, sums)
 
         sums = lax.fori_loop(split, bands, step, (zero,) * 3, unroll=True)
-        if j in mixed:
-            sums = lax.fori_loop(split - jnp.where(plain_ahead, 0, 1), split, step, sums)
+        if j < max(MIXED):
+            sums = lax.fori_loop(split - shifted(wraps_ahead, j), split, step, sums)
         n34, f24, f35 = sums
         zsend[j, 2, first] += -f24
         zsend[j, 2, second] += 8.0 * n34 - f35
@@ -322,9 +322,10 @@
             far = fields_of(lambda n, q, p: inner[j, n, q, p].astype(jnp.float32), n)
             return bonds(n, far, fields_of(at_home(j), n), sums)
 
-        sums = lax.fori_loop(0, last_passed[j], step, (zero,) * 3, unroll=True)
-        if j in mixed:
-            sums = lax.fori_loop(split - jnp.where(plain_behind, 1, 0), split, step, sums)
+        always = split - (j < max(MIXED))
+        sums = lax.fori_loop(0, always, step, (zero,) * 3, unroll=True)
+        if j < max(MIXED):
+            sums = lax.fori_loop(always, split - shifted(wraps, j), step, sums)
         n10, f20, f11 = sums
         zsend[j, 0, first] += 8.0 * n10 - f20
         zsend[j, 0, second] += -f11
@@ -336,7 +337,7 @@
         return pltpu.make_async_remote_copy(
             src_ref=zsend.at[j, role],
             dst_ref=inbox.at[role, slot],
-            send_sem=inbox_send,
+            send_sem=sent,
             recv_sem=inbox_recv.at[role % 2 + role // 3],
             device_id={"band": j, "grid": g},
         )
@@ -345,7 +346,7 @@
         return pltpu.make_async_remote_copy(
             src_ref=zsend.at[j, role],
             dst_ref=final.at[role * nb + b],
-            send_sem=final_send,
+            send_sem=sent,
             recv_sem=final_recv,
             device_id={"band": j, "grid": (g, side, partner, ahead)[role]},
         )
@@ -354,10 +355,10 @@
         to_mate(j, 1).wait_recv()
 
     def arrive_outer(j):
-        by_wrap(plain_ahead, j, lambda start: to_outer(j, start).wait_recv())
+        by_wrap(wraps_ahead, j, lambda start: to_outer(j, start).wait_recv())
 
     def arrive_inner(j):
-        by_wrap(plain_behind, j, lambda stop: to_inner(j, stop).wait_recv())
+        by_wrap(wraps, j, lambda stop: to_inner(j, stop).wait_recv())
 
     def finish(j):
         @pl.when(b == j)
@@ -466,26 +467,16 @@
         out_ref[0, :, near, :] = (zsend[b, 0] + final[3 * nb + b]) * (1.0 / 12.0)
         out_ref[0, :, away, :] = (final[2 * nb + b] + final[nb + b]) * (1.0 / 12.0)
 
-    bytes_of(plane_recv, plane_send_sem).wait_send()
-    bytes_of(mate, mate_send).wait_send()
-    bytes_of(outer.at[pl.ds(MIXED, nb - MIXED), pl.ds(1, bands - split)], outer_send.at[0]).wait_send()
-    bytes_of(inner.at[pl.ds(MIXED, nb - MIXED)], inner_send.at[0]).wait_send()
-    if MIXED:
-        whole = pl.ds(0, MIXED)
-        by_wrap(plain_behind, 0, lambda start: bytes_of(
-            outer.at[whole, pl.ds(start - split + 1, bands - start)], outer_send.at[1]).wait_send())
-        by_wrap(plain_ahead, 0, lambda stop: bytes_of(inner.at[whole, pl.ds(0, stop)], inner_send.at[1]).wait_send())
-    direct = 4 * (nb - relayed)
-
-    @pl.when(b >= relayed)
-    def _():
-        bytes_of(zsend.at[pl.ds(0, relayed)], inbox_send).wait_send()
-        bytes_of(final.at[pl.ds(0, direct - 1)], final_send).wait_send()
-
-    @pl.when(b < relayed)
-    def _():
-        bytes_of(zsend.at[pl.ds(0, relayed - 1)], inbox_send).wait_send()
-        bytes_of(final.at[pl.ds(0, direct + 3)], final_send).wait_send()
+    units = 2 * nb * bands + 8 * nb - 5
+    for parity in (0, 1):
+        for extra, case in (
+            (-MIXED[parity], wraps),
+            (MIXED[parity], wraps_ahead),
+            (0, jnp.logical_not(wraps | wraps_ahead)),
+        ):
+            @pl.when((odd == parity) & case)
+            def _():
+                bytes_of(measure.at[pl.ds(0, units + extra)], sent).wait_send()
 
 
 def solution(mesh):
@@ -521,22 +512,16 @@
                 pltpu.VMEM((nb, 4, depth, half, ny), f32),
                 pltpu.VMEM((4, nb - 1, depth, half, ny), f32),
                 pltpu.VMEM((4 * nb, depth, half, ny), f32),
+                pltpu.VMEM((2 * nb * bands + 8 * nb - 5 + max(MIXED), depth, half, ny), f32),
                 dma,
                 dma,
                 dma,
                 dma((2, nb)),
-                dma((2,)),
                 dma((nb,)),
-                dma((2,)),
                 dma((nb,)),
-                dma,
-                dma,
                 dma,
                 dma((3,)),
                 dma,
-                dma,
-                pltpu.SemaphoreType.REGULAR,
-                pltpu.SemaphoreType.REGULAR,
                 pltpu.SemaphoreType.REGULAR,
                 pltpu.SemaphoreType.REGULAR,
             ],

time: 32.6 us -> 32.2 us (0.988)
  no operation moved by 1% of the time
where the time goes in v6:
time: 32.2 us; the launch traced here: 32 us
  Pallas kernels  31.3 us (97%)
  local copies, waits for them, and re-layouts  0.64 us (2%)
    pallas_call x1, Pallas kernels, per_device(): pl.pallas_call(functools.partial(kernel, nb, ng), out_shape=jax.ShapeDtyp...  31.3 us

profile of v6, /device:TPU:1, one launch (start us, length us, event | category | flops | bytes accessed | tf_op | source)
XLA Modules:
  0.0 32.0 jit_solution(3489825268256156284)
XLA Ops:
  0.0 31.3 %current.1 = f32[3,2,32,128]{3,2,1,0:T(8,128)S(1)} custom-call(f32[16]{0:T(128)} %occ_hbm.1, bf16[16,2,2,128,128]{4,3,2,1,0:T(8,128)(2,1)} %orb_ref.1), custom_call_target="tpu_custom_call" | custom-call | tf_op jit(solution)/shard_map/current/pallas_call | solution.py:494
  31.4 0.6 %copy.4 = f32[3,2,32,128]{3,2,1,0:T(8,128)} copy(f32[3,2,32,128]{3,2,1,0:T(8,128)S(1)} %current.1) | data formatting | bytes 196608

commit v7 on v6

--- a/solution.py
+++ b/solution.py
@@ -26,7 +26,7 @@
 def kernel(
     nb, ng, occ_hbm, orb_ref, out_ref,
     occ_ref, own, mate, outer, inner, mx, my, plane_sum, plane_recv, zsend, inbox, final, measure,
-    occ_sem, own_sem, sent, mate_recv, outer_recv, inner_recv, plane_recv_sem, inbox_recv, final_recv, answers, wrap_in,
+    own_sem, sent, mate_recv, outer_recv, inner_recv, plane_recv_sem, inbox_recv, final_recv, answers, wrap_in,
 ):
     bands, _, depth, nx, ny = orb_ref.shape
     b = lax.axis_index("band")
@@ -46,8 +46,7 @@
 
     load = pltpu.make_async_copy(orb_ref, own, own_sem)
     load.start()
-    weights = pltpu.make_async_copy(occ_hbm, occ_ref, occ_sem)
-    weights.start()
+    weights = pltpu.make_async_copy(occ_hbm, occ_ref, own_sem)
 
     barrier = pltpu.get_barrier_semaphore()
     last = layers - 1
@@ -184,6 +183,7 @@
         by_wrap(wraps, 0, lambda start: to_outer(0, start, orb_ref).start())
 
     load.wait()
+    weights.start()
 
     @pl.when(known)
     def _():
@@ -253,10 +253,13 @@
         to_mate(j, 0).wait_recv()
         by_wrap(wraps_ahead, j, lambda stop: to_inner(j, stop).start())
 
-    @pl.when(wraps_ahead)
-    def _():
-        for j in range(nb - HELD, nb):
-            by_wrap(wraps, j, lambda start: to_outer(j, start).start())
+    def start_held(now):
+        @pl.when(wraps_ahead & now)
+        def _():
+            for j in range(nb - HELD, nb):
+                by_wrap(wraps, j, lambda start: to_outer(j, start).start())
+
+    start_held(b > 0)
 
     mine = pl.ds(pl.multiple_of(b * rows, rows), rows)
     summed = plane_sum[:, :, mine, :]
@@ -390,6 +393,8 @@
 
         if j:
             finish(j - 1)
+            if j == 1:
+                start_held(b == 0)
 
     def send_own(j):
         @pl.when(b != j)
@@ -515,7 +520,6 @@
                 pltpu.VMEM((2 * nb * bands + 8 * nb - 5 + max(MIXED), depth, half, ny), f32),
                 dma,
                 dma,
-                dma,
                 dma((2, nb)),
                 dma((nb,)),
                 dma((nb,)),

time: 32.2 us -> 32.2 us (level)
  no operation moved by 1% of the time
where the time goes in v7:
time: 32.2 us; the launch traced here: 32 us
  Pallas kernels  31.3 us (97%)
  local copies, waits for them, and re-layouts  0.64 us (2%)
    pallas_call x1, Pallas kernels, per_device(): pl.pallas_call(functools.partial(kernel, nb, ng), out_shape=jax.ShapeDtyp...  31.3 us

profile of v7, /device:TPU:1, one launch (start us, length us, event | category | flops | bytes accessed | tf_op | source)
XLA Modules:
  0.0 32.0 jit_solution(324836197167941563)
XLA Ops:
  0.0 31.3 %current.1 = f32[3,2,32,128]{3,2,1,0:T(8,128)S(1)} custom-call(f32[16]{0:T(128)} %occ_hbm.1, bf16[16,2,2,128,128]{4,3,2,1,0:T(8,128)(2,1)} %orb_ref.1), custom_call_target="tpu_custom_call" | custom-call | tf_op jit(solution)/shard_map/current/pallas_call | solution.py:499
  31.3 0.6 %copy.4 = f32[3,2,32,128]{3,2,1,0:T(8,128)} copy(f32[3,2,32,128]{3,2,1,0:T(8,128)S(1)} %current.1) | data formatting | bytes 196608

commit v8 on v7

--- a/solution.py
+++ b/solution.py
@@ -259,7 +259,7 @@
             for j in range(nb - HELD, nb):
                 by_wrap(wraps, j, lambda start: to_outer(j, start).start())
 
-    start_held(b > 0)
+    start_held((b > 0) | (odd == 1))
 
     mine = pl.ds(pl.multiple_of(b * rows, rows), rows)
     summed = plane_sum[:, :, mine, :]
@@ -394,7 +394,7 @@
         if j:
             finish(j - 1)
             if j == 1:
-                start_held(b == 0)
+                start_held((b == 0) & (odd == 0))
 
     def send_own(j):
         @pl.when(b != j)

time: 32.2 us -> 32.1 us (level)
  no operation moved by 1% of the time
where the time goes in v8:
time: 32.1 us; the launch traced here: 32 us
  Pallas kernels  31.3 us (98%)
  local copies, waits for them, and re-layouts  0.64 us (2%)
    pallas_call x1, Pallas kernels, per_device(): pl.pallas_call(functools.partial(kernel, nb, ng), out_shape=jax.ShapeDtyp...  31.3 us
    unnamed x1, local copies, waits for them, and re-layouts  0.64 us

profile of v8, /device:TPU:1, one launch (start us, length us, event | category | flops | bytes accessed | tf_op | source)
XLA Modules:
  0.0 32.0 jit_solution(111110210264127463)
XLA Ops:
  0.0 31.3 %current.1 = f32[3,2,32,128]{3,2,1,0:T(8,128)S(1)} custom-call(f32[16]{0:T(128)} %occ_hbm.1, bf16[16,2,2,128,128]{4,3,2,1,0:T(8,128)(2,1)} %orb_ref.1), custom_call_target="tpu_custom_call" | custom-call | tf_op jit(solution)/shard_map/current/pallas_call | solution.py:499
  31.3 0.6 %copy.4 = f32[3,2,32,128]{3,2,1,0:T(8,128)} copy(f32[3,2,32,128]{3,2,1,0:T(8,128)S(1)} %current.1) | data formatting | bytes 196608
